TPU v7x, 8 devices: a whole 2x2x1 slice. The times are simulated.
8 devices in a mesh: data: 1 (over z), cp: 2 (over y), tp: 4 (over x, core).
Axes of the slice: x: 2, y: 2, z: 1, core: 2. Of those that a mesh axis runs over, the one named last changes fastest.
Arguments:
- x_in: bfloat16 [4096, 2048], P(('data', 'cp', 'tp'))
- w_q: bfloat16 [2048, 16, 128], P(None, 'tp')
- w_k: bfloat16 [2048, 16, 128], P(None, 'tp')
- w_v: bfloat16 [2048, 16, 128], P(None, 'tp')
- w_o: bfloat16 [16, 128, 2048], P('tp')
- expert_idx: int32 [4096, 2], P(('data', 'cp', 'tp'))
- gate_wts: float32 [4096, 2], P(('data', 'cp', 'tp'))
- w_gate: bfloat16 [64, 2048, 1024], P(('cp', 'tp'))
- w_up: bfloat16 [64, 2048, 1024], P(('cp', 'tp'))
- w_down: bfloat16 [64, 1024, 2048], P(('cp', 'tp'))
Outputs:
- output: bfloat16 [4096, 2048], P(('data', 'cp', 'tp'))
All inputs are finite; a program needn't handle non-finite values.
Results may differ from a plain program's by a relative error of at most 0.0146932.
Values are sent between devices in bfloat16 or wider.
A program may use at most 1 GiB of HBM per device.

v0:
```python
import jax
import jax.numpy as jnp
from jax import lax
from jax.sharding import PartitionSpec as P


def row_positions(cp_ranks, cp_size, tp_size, tok_dev):
    half_rows = tok_dev // 2
    local_rows = jnp.arange(tp_size * tok_dev)
    tp_src = local_rows // tok_dev
    within = local_rows % tok_dev
    seg_index = jnp.where((within < half_rows)[None, :], cp_ranks[:, None], 2 * cp_size - 1 - cp_ranks[:, None])
    offset = tp_src * half_rows + within % half_rows
    return (seg_index * (tp_size * half_rows) + offset[None, :]).reshape(-1)


def solution(mesh):
    cp_size = mesh.shape['cp']
    tp_size = mesh.shape['tp']
    num_devs = cp_size * tp_size
    row_spec = P(('data', 'cp', 'tp'), None)
    head_spec = P(None, 'tp', None)
    wo_spec = P('tp', None, None)
    expert_spec = P(('cp', 'tp'), None, None)

    def device_fn(x_blk, w_q, w_k, w_v, w_o, idx_blk, gate_blk, w_gate, w_up, w_down):
        tok_dev = x_blk.shape[0]
        kv_local, head_dim = w_k.shape[1], w_k.shape[2]
        q_per_kv = w_q.shape[1] // kv_local
        exp_local = w_gate.shape[0]
        num_exp = exp_local * num_devs
        capacity = 4 * tok_dev // num_exp
        cp_rank = lax.axis_index('cp')

        x_rows = lax.all_gather(x_blk, 'tp', axis=0, tiled=True)
        queries = jnp.einsum('sm,mnc->snc', x_rows, w_q, preferred_element_type=jnp.float32).astype(jnp.bfloat16)
        keys_loc = jnp.einsum('sm,mnc->snc', x_rows, w_k, preferred_element_type=jnp.float32).astype(jnp.bfloat16)
        vals_loc = jnp.einsum('sm,mnc->snc', x_rows, w_v, preferred_element_type=jnp.float32).astype(jnp.bfloat16)
        keys_all = lax.all_gather(keys_loc, 'cp', axis=0, tiled=True)
        vals_all = lax.all_gather(vals_loc, 'cp', axis=0, tiled=True)
        pos_q = row_positions(cp_rank.reshape(1), cp_size, tp_size, tok_dev)
        pos_k = row_positions(jnp.arange(cp_size), cp_size, tp_size, tok_dev)
        q_grp = queries.reshape(-1, kv_local, q_per_kv, head_dim)
        scores = jnp.einsum('qngc,knc->ngqk', q_grp, keys_all, preferred_element_type=jnp.float32) * (head_dim ** -0.5)
        scores = jnp.where(pos_k[None, None, None, :] <= pos_q[None, None, :, None], scores, -jnp.inf)
        exp_scores = jnp.exp(scores - jnp.max(scores, axis=-1, keepdims=True))
        attn_prob = (exp_scores / jnp.sum(exp_scores, axis=-1, keepdims=True)).astype(jnp.bfloat16)
        head_out = jnp.einsum('ngqk,knc->qngc', attn_prob, vals_all, preferred_element_type=jnp.float32).astype(jnp.bfloat16)
        part_sum = jnp.einsum('qngc,ngcm->qm', head_out, w_o.reshape(kv_local, q_per_kv, head_dim, -1), preferred_element_type=jnp.float32)
        attn_out = lax.psum_scatter(part_sum, 'tp', scatter_dimension=0, tiled=True)
        hidden = (x_blk.astype(jnp.float32) + attn_out).astype(jnp.bfloat16)

        flat_ids = idx_blk.reshape(-1)
        onehot = (flat_ids[:, None] == jnp.arange(num_exp)[None, :]).astype(jnp.int32)
        slot_pos = jnp.sum(jnp.cumsum(onehot, axis=0) * onehot, axis=1) - 1
        slot_ids = (flat_ids * capacity + slot_pos).reshape(tok_dev, 2)
        select = (slot_ids[:, :, None] == jnp.arange(num_exp * capacity)[None, None, :]).astype(jnp.bfloat16)
        send_buf = jnp.einsum('tkn,tm->nm', select, hidden, preferred_element_type=jnp.float32).astype(jnp.bfloat16)
        recv_buf = lax.all_to_all(send_buf, ('cp', 'tp'), 0, 0, tiled=True)
        tok_in = recv_buf.reshape(num_devs, exp_local, capacity, -1)
        gate_pre = jnp.einsum('secm,emf->secf', tok_in, w_gate, preferred_element_type=jnp.float32)
        up_pre = jnp.einsum('secm,emf->secf', tok_in, w_up, preferred_element_type=jnp.float32)
        hid_act = (jax.nn.silu(gate_pre) * up_pre).astype(jnp.bfloat16)
        exp_out = jnp.einsum('secf,efm->secm', hid_act, w_down, preferred_element_type=jnp.float32).astype(jnp.bfloat16)
        back_buf = lax.all_to_all(exp_out.reshape(num_devs * exp_local * capacity, -1), ('cp', 'tp'), 0, 0, tiled=True)
        picked = jnp.einsum('tkn,nm->tkm', select, back_buf, preferred_element_type=jnp.float32)
        moe_out = jnp.sum(gate_blk[:, :, None] * picked, axis=1)
        return (hidden.astype(jnp.float32) + moe_out).astype(jnp.bfloat16)

    return jax.shard_map(device_fn, mesh=mesh, in_specs=(row_spec, head_spec, head_spec, head_spec, wo_spec, row_spec, row_spec, expert_spec, expert_spec, expert_spec), out_specs=row_spec, check_vma=False)
```

profile of v0, /device:TPU:0, one launch (start us, length us, event | category | flops | bytes accessed | tf_op | source)
XLA Modules:
  0.0 697.8 jit_solution(10682520026791140354)
XLA Ops:
  6.5 0.0 copy-start
  6.5 0.0 all-gather.4.cloned.1.call-start
  6.5 0.7 all-gather.4.cloned.1.call-update
  7.3 0.0 all-gather.8.cloned.1.call-start
  7.3 60.1 %all-gather.4.cloned.1.call-done = bf16[2048,2048]{1,0:T(8,128)(2,1)} async-done(((bf16[512,2048]{1,0:T(8,128)(2,1)}), bf16[2048,2048]{1,0:T(8,128)(2,1)}) %all-gather.4.cloned.1.call-update) | async-done | bytes 8388624 | tf_op jit(solution)/shard_map/all_gather | solution.py:35
  67.4 9.9 %fusion.34 = bf16[2048,4,128]{2,0,1:T(8,128)(2,1)} fusion(bf16[2048,2048]{1,0:T(8,128)(2,1)} %all-gather.4.cloned.1.call-done, bf16[2048,4,128]{2,1,0:T(4,128)(2,1)} %param.12), kind=kOutput, calls=%fused_computation.41 | convolution fusion | flops 4296015872 | bytes 12582912 | tf_op jit(solution)/shard_map/sm,mnc->snc/dot_general | solution.py:37
  77.3 0.0 all-gather.8.cloned.1.call-update
  77.4 0.0 all-gather.6.cloned.1.call-start
  77.5 0.1 add_bitcast_fusion
  77.5 0.0 copy-start.4
  77.6 7.6 %broadcast_compare_fusion = pred[2048,4096]{0,1:T(8,128)(4,1)} fusion(s32[2048]{0:T(1024)S(1)} %multiply_add_fusion, s32[4096]{0:T(1024)S(1)} %bitcast.140), kind=kLoop, calls=%fused_computation.13 | loop fusion | flops 8388608 | bytes 8413184 | tf_op jit(solution)/shard_map/le | solution.py:45
  85.2 0.0 copy-done.4
  85.2 7.3 %fusion.31 = bf16[2048,4,128]{2,0,1:T(8,128)(2,1)} fusion(bf16[2048,2048]{1,0:T(8,128)(2,1)S(1)} %copy-done.4, bf16[2048,4,128]{2,1,0:T(4,128)(2,1)} %param.13), kind=kOutput, calls=%fused_computation.40 | convolution fusion | flops 4296015872 | bytes 12582912 | tf_op jit(solution)/shard_map/sm,mnc->snc/dot_general | solution.py:38
  92.4 0.0 all-gather.6.cloned.1.call-update
  92.5 0.0 reduce-scatter.2.cloned.1.call-start
  92.5 9.9 %fusion.37 = bf16[2048,4,128]{2,0,1:T(8,128)(2,1)} fusion(bf16[2048,2048]{1,0:T(8,128)(2,1)} %all-gather.4.cloned.1.call-done, bf16[2048,4,128]{2,1,0:T(4,128)(2,1)} %param.11), kind=kOutput, calls=%fused_computation.42 | convolution fusion | flops 4296015872 | bytes 12582912 | tf_op jit(solution)/shard_map/sm,mnc->snc/dot_general | solution.py:36
  102.4 29.3 %all-gather.8.cloned.1.call-done = bf16[4096,4,128]{2,0,1:T(8,128)(2,1)} async-done(((bf16[2048,4,128]{2,0,1:T(8,128)(2,1)}), bf16[4096,4,128]{2,0,1:T(8,128)(2,1)}) %all-gather.8.cloned.1.call-update) | async-done | bytes 4194320 | tf_op jit(solution)/shard_map/all_gather | solution.py:39
  131.7 50.7 %fusion.1 = (f32[4,2048]{1,0:T(4,128)S(1)}, f32[4,4096,2048]{2,1,0:T(8,128)}) fusion(pred[2048,4096]{0,1:T(8,128)(4,1)} %broadcast_compare_fusion, bf16[4096,4,128]{2,0,1:T(8,128)(2,1)} %all-gather.8.cloned.1.call-done, bf16[2048,4,128]{2,0,1:T(8,128)(2,1)} %fusion.37), kind=kOutput, calls=%fused_computation.4 | convolution fusion | flops 8690589696 | bytes 148930560 | tf_op jit(solution)/shard_map/qngc,knc->ngqk/dot_general | solution.py:44
  182.4 43.8 %fusion = f32[4,2048]{1,0:T(4,128)S(1)} fusion(f32[4,4096,2048]{2,1,0:T(8,128)} %get-tuple-element.6, f32[4,2048]{1,0:T(4,128)S(1)} %get-tuple-element.5, pred[2048,4096]{0,1:T(8,128)(4,1)} %broadcast_compare_fusion), kind=kLoop, calls=%fused_computation.3 | loop fusion | flops 134209536 | bytes 142671872 | tf_op jit(solution)/shard_map/reduce_sum | solution.py:47
  226.2 0.0 all-gather.6.cloned.1.call-done
  226.2 52.9 %fusion.43.clone.4 = bf16[2048,4,128]{0,2,1:T(8,128)(2,1)} fusion(bf16[4096,4,128]{2,0,1:T(8,128)(2,1)} %all-gather.6.cloned.1.call-done, f32[4,2048]{1,0:T(4,128)S(1)} %fusion, f32[4,2048]{1,0:T(4,128)S(1)} %get-tuple-element.5, f32[4,4096,2048]{2,1,0:T(8,128)} %get-tuple-element.6, pred[2048,4096]{0,1:T(8,128)(4,1)} %broadcast_compare_fusion), kind=kOutput, calls=%fused_computation.44.clone.clone.clone.1 | convolution fusion | flops 8758755328 | bytes 148963328 | tf_op jit(solution)/shard_map/ngqk,knc->qngc/dot_general | solution.py:48
  279.1 0.0 copy-done
  279.1 9.8 %convolution_bitcast_fusion = f32[2048,2048]{1,0:T(8,128)} fusion(bf16[4,128,2048]{2,1,0:T(8,128)(2,1)S(1)} %copy-done, bf16[2048,4,128]{0,2,1:T(8,128)(2,1)} %fusion.43.clone.4), kind=kOutput, calls=%fused_computation.14 | convolution fusion | flops 4294967296 | bytes 20971520 | tf_op jit(solution)/shard_map/qngc,ngcm->qm/dot_general | solution.py:49
  288.9 0.0 copy-start.3
  289.0 0.0 reduce-scatter.2.cloned.1.call-update
  289.0 0.7 copy-done.3
  289.6 0.1 copy.30
  289.8 0.2 eq.47
  290.0 0.2 eq.43
  290.2 18.0 %reduce-window.6 = s32[64,8,128]{2,1,0:T(8,128)S(1)} reduce-window(s32[64,8,128]{2,1,0:T(8,128)S(1)} %fusion.53, s32[]{:T(128)} %constant.73.clone.1), window={size=1x1x128 pad=0_0x0_0x127_0}, to_apply=%region_3.4 | reduce-window | flops 8323072 | bytes 524292 | tf_op jit(solution)/shard_map/reduce-window
  308.2 0.1 slice.8
  308.3 0.1 copy.32
  308.5 0.1 copy.33
  308.6 0.1 broadcast_add_fusion
  308.7 0.1 fusion.52
  308.8 0.2 sub.42
  309.0 0.1 copy.34
  309.1 2.4 convert_reduce_fusion
  311.5 96.5 %reduce-scatter.2.cloned.1.call-done = f32[512,2048]{1,0:T(8,128)} async-done(((f32[2048,2048]{1,0:T(8,128)}), f32[512,2048]{1,0:T(8,128)}) %reduce-scatter.2.cloned.1.call-update) | async-done | bytes 4194320 | tf_op jit(solution)/shard_map/reduce_scatter | solution.py:50
  408.0 8.1 %convolution_convert_fusion = bf16[2048,2048]{1,0:T(8,128)(2,1)S(1)} fusion(bf16[512,2048]{1,0:T(8,128)(2,1)} %convert_reduce_fusion, f32[512,2048]{1,0:T(8,128)} %reduce-scatter.2.cloned.1.call-done, bf16[512,2048]{1,0:T(8,128)(2,1)} %param.10), kind=kOutput, calls=%fused_computation.34 | convolution fusion | flops 4298113024 | bytes 16777216 | tf_op jit(solution)/shard_map/tkn,tm->nm/dot_general | solution.py:58
  416.0 96.3 %all_to_all.21 = bf16[8,256,2048]{2,1,0:T(8,128)(2,1)} all-to-all(bf16[8,256,2048]{2,1,0:T(8,128)(2,1)S(1)} %bitcast.138), channel_id=1, replica_groups=mesh['data'=1,'cp'=2,'tp'=4] {'cp','tp'}, dimensions={0} | all-to-all | bytes 16777216 | tf_op jit(solution)/shard_map/all_to_all | solution.py:59
  512.4 22.8 %fusion.6 = f32[8,8,32,1024]{3,2,1,0:T(8,128)} fusion(bf16[8,2048,1024]{2,1,0:T(8,128)(2,1)} %param.18, bf16[8,8,32,2048]{3,2,1,0:T(8,128)(2,1)} %bitcast.135), kind=kOutput, calls=%fused_computation.9 | convolution fusion | flops 8589934592 | bytes 50331648 | tf_op jit(solution)/shard_map/secm,emf->secf/dot_general | solution.py:62
  535.2 20.4 %fusion.10 = bf16[8,8,32,1024]{3,2,0,1:T(8,128)(2,1)} fusion(f32[8,8,32,1024]{3,2,1,0:T(8,128)} %fusion.6, bf16[8,2048,1024]{2,1,0:T(8,128)(2,1)} %param.17, bf16[8,8,32,2048]{3,2,1,0:T(8,128)(2,1)} %bitcast.136), kind=kOutput, calls=%fused_computation.16 | convolution fusion | flops 8602517504 | bytes 54525952 | tf_op jit(solution)/shard_map/secm,emf->secf/dot_general | solution.py:61
  555.6 18.3 %convert_bitcast_fusion = bf16[8,8,32,2048]{3,2,0,1:T(8,128)(2,1)} fusion(bf16[8,8,32,1024]{3,2,0,1:T(8,128)(2,1)} %fusion.10, bf16[8,1024,2048]{2,1,0:T(8,128)(2,1)} %param.19), kind=kOutput, calls=%fused_computation.29 | convolution fusion | flops 8594128896 | bytes 46137344 | tf_op jit(solution)/shard_map/secf,efm->secm/dot_general | solution.py:64
  573.8 8.3 %copy.37 = bf16[8,8,32,2048]{3,2,1,0:T(8,128)(2,1)} copy(bf16[8,8,32,2048]{3,2,0,1:T(8,128)(2,1)} %convert_bitcast_fusion) | data formatting | bytes 16777216 | tf_op jit(solution)/shard_map/convert_element_type | solution.py:64
  582.1 0.0 copy-start.5
  582.1 96.7 %all_to_all.22 = bf16[8,256,2048]{2,1,0:T(8,128)(2,1)S(1)} all-to-all(bf16[8,256,2048]{2,1,0:T(8,128)(2,1)} %bitcast.134), channel_id=1, replica_groups=mesh['data'=1,'cp'=2,'tp'=4] {'cp','tp'}, dimensions={0} | all-to-all | bytes 16777216 | tf_op jit(solution)/shard_map/all_to_all | solution.py:65
  678.8 0.0 copy-done.5
  678.8 0.0 copy-start.1
  678.8 0.0 copy-start.2
  678.8 9.4 %multiply_reduce_fusion = f32[512,2048]{1,0:T(8,128)S(1)} fusion(f32[512,2]{0,1:T(2,128)S(1)} %copy-done.5, bf16[2048,2048,1]{1,0,2:T(8,128)(2,1)S(1)} %bitcast.137, s32[512,2]{0,1:T(2,128)S(1)} %multiply_add_fusion.1), kind=kOutput, calls=%fused_computation.28 | convolution fusion | flops 8595177472 | bytes 12591104 | tf_op jit(solution)/shard_map/tkn,nm->tkm/dot_general | solution.py:66
  688.3 0.0 copy-done.1
  688.3 0.0 copy-done.2
  688.3 2.5 add_convert_fusion
  (10 shorter events, 0.1 us)
Async XLA Ops:
  6.5 272.6 %copy-start = (bf16[4,128,2048]{2,1,0:T(8,128)(2,1)S(1)}, bf16[4,128,2048]{2,1,0:T(8,128)(2,1)}, u32[]{:S(2)}) copy-start(bf16[4,128,2048]{2,1,0:T(8,128)(2,1)} %param.14) | copy-start | bytes 6291460
  6.5 60.9 %all-gather.4.cloned.1.call-start = ((), (), s32[]{:S(2)}) async-start(), calls=%async_computation.3 | async-start | bytes 10485760 | tf_op jit(solution)/shard_map/all_gather | solution.py:35
  7.3 124.4 %all-gather.8.cloned.1.call-start = ((), (), s32[]{:S(2)}) async-start(), calls=%async_computation.5 | async-start | bytes 6291456 | tf_op jit(solution)/shard_map/all_gather | solution.py:39
  77.4 148.8 %all-gather.6.cloned.1.call-start = ((), (), s32[]{:S(2)}) async-start(), calls=%async_computation.4 | async-start | bytes 6291456 | tf_op jit(solution)/shard_map/all_gather | solution.py:40
  77.5 7.6 %copy-start.4 = (bf16[2048,2048]{1,0:T(8,128)(2,1)S(1)}, bf16[2048,2048]{1,0:T(8,128)(2,1)}, u32[]{:S(2)}) copy-start(bf16[2048,2048]{1,0:T(8,128)(2,1)} %all-gather.4.cloned.1.call-done) | copy-start | bytes 25165828
  92.5 315.5 %reduce-scatter.2.cloned.1.call-start = ((), (), s32[]{:S(2)}) async-start(), calls=%async_computation.6 | async-start | bytes 20971520 | tf_op jit(solution)/shard_map/reduce_scatter | solution.py:50
  288.9 0.7 copy-start.3
  582.1 96.7 %copy-start.5 = (f32[512,2]{0,1:T(2,128)S(1)}, f32[512,2]{0,1:T(2,128)}, u32[]{:S(2)}) copy-start(f32[512,2]{0,1:T(2,128)} %param.16) | copy-start | bytes 12292
  678.8 9.5 %copy-start.1 = (bf16[512,2048]{1,0:T(8,128)(2,1)S(1)}, bf16[512,2048]{1,0:T(8,128)(2,1)}, u32[]{:S(2)}) copy-start(bf16[512,2048]{1,0:T(8,128)(2,1)} %param.10) | copy-start | bytes 6291460
  678.8 9.5 %copy-start.2 = (f32[512,2048]{1,0:T(8,128)S(1)}, f32[512,2048]{1,0:T(8,128)}, u32[]{:S(2)}) copy-start(f32[512,2048]{1,0:T(8,128)} %reduce-scatter.2.cloned.1.call-done) | copy-start | bytes 12582916
Sparse Core Ops, SparseCore 0:
  8.9 58.5 all-gather.3
  77.5 54.1 all-gather.7
  133.2 54.1 all-gather.5
  289.1 118.8 reduce-scatter.1
where the time goes:
time: 706 us; the launch traced here: 698 us
  matrix products  219 us (31%)
  blocking collectives  193 us (27%)
  waiting for transfers between devices  187 us (26%)
  other arithmetic  74.7 us (11%)
  between operations  13.7 us (2%)
  local copies, waits for them, and re-layouts  10.1 us (1%)
    all_to_all x1, blocking collectives, device_fn(): lax.all_to_all(exp_out.reshape(num_devs * exp_local * capacity, -1), ('cp...  96.7 us
    reduce_scatter x1, waiting for transfers between devices, device_fn(): attn_out = lax.psum_scatter(part_sum, 'tp', scatter_dimension=0, tiled=True)  96.5 us
    all_to_all x1, blocking collectives, device_fn(): recv_buf = lax.all_to_all(send_buf, ('cp', 'tp'), 0, 0, tiled=True)  96.3 us
    all_gather x1, waiting for transfers between devices, device_fn(): x_rows = lax.all_gather(x_blk, 'tp', axis=0, tiled=True)  60.1 us
    dot_general x1, matrix products, device_fn(): jnp.einsum('ngqk,knc->qngc', attn_prob, vals_all, preferred_element_type=...  52.9 us
    dot_general x1, matrix products, device_fn(): jnp.einsum('qngc,knc->ngqk', q_grp, keys_all, preferred_element_type=jnp....  50.7 us
    reduce_sum x1, other arithmetic, device_fn(): jnp.sum(exp_scores, axis=-1, keepdims=True)  43.8 us
    all_gather x1, waiting for transfers between devices, device_fn(): keys_all = lax.all_gather(keys_loc, 'cp', axis=0, tiled=True)  29.3 us
  transfers between devices with their start and end apart: 4, of which 3 were waited for; matrix products, arithmetic and copies ran while one was open for 20% of the time, Pallas kernels for 0%

commit v1 on v0

v1 whole, which is shorter than its diff:
```python
import functools
import math

import jax
import jax.numpy as jnp
from jax import lax
from jax.experimental import pallas as pl
from jax.experimental.pallas import tpu as pltpu
from jax.sharding import PartitionSpec as P

QB = 512


def attn_kernel(q_ref, k_ref, v_ref, o_ref, s_ref, acc_ref, *, heads, head_dim, seq):
    coef = (head_dim ** -0.5) * math.log2(math.e)
    lane = 128
    groups = QB // lane

    def lane_max(s):
        out = s[:, :lane]
        for g in range(1, groups):
            out = jnp.maximum(out, s[:, g * lane:(g + 1) * lane])
        return out

    def lane_sum(s):
        out = s[:, :lane]
        for g in range(1, groups):
            out = out + s[:, g * lane:(g + 1) * lane]
        return out

    for h in range(heads):
        cols = slice(h * head_dim, (h + 1) * head_dim)

        def q_step(i, _):
            q_rows = pl.ds(pl.multiple_of(i * QB, QB), QB)
            q = q_ref[q_rows, cols]

            def scores(j):
                k = k_ref[pl.ds(pl.multiple_of(j * QB, QB), QB), cols]
                return lax.dot_general(q, k, (((1,), (1,)), ((), ())), preferred_element_type=jnp.float32)

            def pass1(j, m):
                s = scores(j)
                s_ref[:, pl.ds(pl.multiple_of(j * QB, QB), QB)] = s
                return jnp.maximum(m, lane_max(s))

            m = lax.fori_loop(0, i, pass1, jnp.full((QB, lane), -jnp.inf, jnp.float32))
            s = scores(i)
            row = lax.broadcasted_iota(jnp.int32, (QB, QB), 0)
            col = lax.broadcasted_iota(jnp.int32, (QB, QB), 1)
            s = jnp.where(col <= row, s, -jnp.inf)
            s_ref[:, pl.ds(pl.multiple_of(i * QB, QB), QB)] = s
            m = jnp.max(jnp.maximum(m, lane_max(s)), axis=1, keepdims=True)
            acc_ref[...] = jnp.zeros_like(acc_ref)

            def pass2(j, l):
                s = s_ref[:, pl.ds(pl.multiple_of(j * QB, QB), QB)]
                e = jnp.exp2((s - m) * coef)
                v = v_ref[pl.ds(pl.multiple_of(j * QB, QB), QB), cols]
                acc_ref[...] += lax.dot_general(e.astype(jnp.bfloat16), v, (((1,), (0,)), ((), ())), preferred_element_type=jnp.float32)
                return l + lane_sum(e)

            l = lax.fori_loop(0, i + 1, pass2, jnp.zeros((QB, lane), jnp.float32))
            l = jnp.sum(l, axis=1, keepdims=True)
            o_ref[q_rows, cols] = (acc_ref[...] / l).astype(jnp.bfloat16)
            return 0

        lax.fori_loop(0, seq // QB, q_step, 0)


def attention(q, k, v, heads, head_dim):
    seq = q.shape[0]
    vm = pl.BlockSpec(memory_space=pltpu.VMEM)
    return pl.pallas_call(
        functools.partial(attn_kernel, heads=heads, head_dim=head_dim, seq=seq),
        out_shape=jax.ShapeDtypeStruct(q.shape, jnp.bfloat16),
        in_specs=[vm] * 3,
        out_specs=vm,
        scratch_shapes=[pltpu.VMEM((QB, seq), jnp.float32), pltpu.VMEM((QB, head_dim), jnp.float32)],
        compiler_params=pltpu.CompilerParams(vmem_limit_bytes=60 * 1024 * 1024),
        cost_estimate=pl.CostEstimate(flops=2 * heads * seq * seq * head_dim, bytes_accessed=4 * 2 * q.size, transcendentals=heads * seq * seq // 2),
    )(q, k, v)


def solution(mesh):
    cp_size = mesh.shape['cp']
    tp_size = mesh.shape['tp']
    num_devs = cp_size * tp_size
    row_spec = P(('data', 'cp', 'tp'), None)
    head_spec = P(None, 'tp', None)
    wo_spec = P('tp', None, None)
    expert_spec = P(('cp', 'tp'), None, None)

    def to_positions(rows, half):
        blocks = rows.reshape(cp_size, tp_size, 2, half, rows.shape[-1])
        return jnp.concatenate([blocks[:, :, 0], blocks[::-1, :, 1]], axis=0).reshape(rows.shape)

    def from_positions(rows, half):
        blocks = rows.reshape(2 * cp_size, tp_size, half, rows.shape[-1])
        return jnp.stack([blocks[:cp_size], blocks[cp_size:][::-1]], axis=2).reshape(rows.shape)

    def device_fn(x_blk, w_q, w_k, w_v, w_o, idx_blk, gate_blk, w_gate, w_up, w_down):
        tok_dev, d_model = x_blk.shape
        half = tok_dev // 2
        heads_tp, head_dim = w_q.shape[1], w_q.shape[2]
        heads = heads_tp // cp_size
        width = heads * head_dim
        exp_local = w_gate.shape[0]
        num_exp = exp_local * num_devs
        capacity = 4 * tok_dev // num_exp
        cp_rank = lax.axis_index('cp')

        x_all = lax.all_gather(x_blk, ('cp', 'tp'), axis=0, tiled=True)
        wo_all = lax.all_gather(w_o, 'tp', axis=0, tiled=True).reshape(-1, d_model)
        w_qkv = jnp.concatenate([lax.dynamic_slice_in_dim(w, cp_rank * heads, heads, 1).reshape(d_model, width) for w in (w_q, w_k, w_v)], axis=1)
        qkv = jnp.dot(x_all, w_qkv, preferred_element_type=jnp.float32).astype(jnp.bfloat16)
        qkv = to_positions(qkv, half)
        o = attention(qkv[:, :width], qkv[:, width:2 * width], qkv[:, 2 * width:], heads, head_dim)
        o = from_positions(o, half)
        o = lax.all_to_all(o, ('cp', 'tp'), 0, 0, tiled=True)
        o = o.reshape(cp_size, tp_size, tok_dev, width).transpose(2, 1, 0, 3).reshape(tok_dev, -1)
        attn_out = jnp.dot(o, wo_all, preferred_element_type=jnp.float32)
        hidden = (x_blk.astype(jnp.float32) + attn_out).astype(jnp.bfloat16)

        flat_ids = idx_blk.reshape(-1)
        num_flat = flat_ids.shape[0]
        onehot = (flat_ids[:, None] == jnp.arange(num_exp)[None, :])
        before = (jnp.arange(num_flat)[:, None] > jnp.arange(num_flat)[None, :]).astype(jnp.bfloat16)
        ranks = jnp.dot(before, onehot.astype(jnp.bfloat16), preferred_element_type=jnp.float32)
        slot_pos = jnp.sum(jnp.where(onehot, ranks, 0.0), axis=1).astype(jnp.int32)
        slot_ids = (flat_ids * capacity + slot_pos).reshape(tok_dev, 2)
        select = (slot_ids[:, :, None] == jnp.arange(num_exp * capacity)[None, None, :]).astype(jnp.bfloat16)
        send_buf = jnp.einsum('tkn,tm->nm', select, hidden, preferred_element_type=jnp.float32).astype(jnp.bfloat16)
        recv_buf = lax.all_to_all(send_buf, ('cp', 'tp'), 0, 0, tiled=True)
        tok_in = recv_buf.reshape(num_devs, exp_local, capacity, -1)
        gate_pre = jnp.einsum('secm,emf->secf', tok_in, w_gate, preferred_element_type=jnp.float32)
        up_pre = jnp.einsum('secm,emf->secf', tok_in, w_up, preferred_element_type=jnp.float32)
        hid_act = (jax.nn.silu(gate_pre) * up_pre).astype(jnp.bfloat16)
        exp_out = jnp.einsum('secf,efm->secm', hid_act, w_down, preferred_element_type=jnp.float32).astype(jnp.bfloat16)
        back_buf = lax.all_to_all(exp_out.reshape(num_devs * exp_local * capacity, -1), ('cp', 'tp'), 0, 0, tiled=True)
        picked = jnp.einsum('tkn,nm->tkm', select, back_buf, preferred_element_type=jnp.float32)
        moe_out = jnp.sum(gate_blk[:, :, None] * picked, axis=1)
        return (hidden.astype(jnp.float32) + moe_out).astype(jnp.bfloat16)

    return jax.shard_map(device_fn, mesh=mesh, in_specs=(row_spec, head_spec, head_spec, head_spec, wo_spec, row_spec, row_spec, expert_spec, expert_spec, expert_spec), out_specs=row_spec, check_vma=False)
```

time: 706 us -> 573 us (0.81)
  matrix products: 219 us -> 105 us
  waiting for transfers between devices: 187 us -> 100 us
  local copies, waits for them, and re-layouts: 10.1 us -> 85.6 us
  other arithmetic: 74.7 us -> 8.36 us
  Pallas kernels: 0 us -> 55.1 us
    dot_general x6 -> x3, matrix products: 140 us -> 28.9 us  [the longest x1 19.1 us: device_fn(): jnp.dot(x_all, w_qkv, preferred_element_type=jnp.float32)]
    reduce_scatter x1 -> x0, waiting for transfers between devices: 96.5 us -> none  [device_fn(): attn_out = lax.psum_scatter(part_sum, 'tp', scatter_dimension=0, tiled=True)]
    pallas_call x0 -> x1, Pallas kernels: none -> 55.1 us  [attention(): pl.pallas_call(functools.partial(attn_kernel, heads=heads, head_dim=head_...]
    reduce_sum x2 -> x0, other arithmetic: 43.9 us -> none  [the longest x1 43.8 us: device_fn(): jnp.sum(exp_scores, axis=-1, keepdims=True)]
    unnamed x14 -> x20, local copies, waits for them, and re-layouts: 0.83 us -> 37.2 us
    all_to_all x0 -> x1, waiting for transfers between devices: none -> 22.9 us  [device_fn(): o = lax.all_to_all(o, ('cp', 'tp'), 0, 0, tiled=True)]
    slice x2 -> x3, local copies, waits for them, and re-layouts: 0.26 us -> 18.4 us  [the longest x1 13.9 us: to_positions(): blocks[:, :, 0]]
    another operation x3 -> x1, other arithmetic: 18.2 us -> 1.52 us  [from_positions(): jnp.stack([blocks[:cp_size], blocks[cp_size:][::-1]], axis=2)]
  transfers between devices with their start and end apart: 4 -> 3, of which waited for: 3 -> 2; matrix products, arithmetic and copies ran while one was open for 20% -> 18% of each run, Pallas kernels for 0% -> 10%
where the time goes in v1:
time: 573 us; the launch traced here: 564 us
  blocking collectives  193 us (34%)
  matrix products  105 us (18%)
  waiting for transfers between devices  100 us (17%)
  local copies, waits for them, and re-layouts  85.6 us (15%)
  Pallas kernels  55.1 us (10%)
  between operations  14 us (2%)
  other arithmetic  8.36 us (1%)
    all_to_all x1, blocking collectives, device_fn(): lax.all_to_all(exp_out.reshape(num_devs * exp_local * capacity, -1), ('cp...  96.7 us
    all_to_all x1, blocking collectives, device_fn(): recv_buf = lax.all_to_all(send_buf, ('cp', 'tp'), 0, 0, tiled=True)  96.3 us
    all_gather x1, waiting for transfers between devices, device_fn(): x_all = lax.all_gather(x_blk, ('cp', 'tp'), axis=0, tiled=True)  75.9 us
    pallas_call x1, Pallas kernels, attention(): pl.pallas_call(functools.partial(attn_kernel, heads=heads, head_dim=head_...  55.1 us
    unnamed x20, local copies, waits for them, and re-layouts  37.2 us
    dot_general x1, matrix products, device_fn(): jnp.einsum('secm,emf->secf', tok_in, w_up, preferred_element_type=jnp.flo...  22.9 us
    all_to_all x1, waiting for transfers between devices, device_fn(): o = lax.all_to_all(o, ('cp', 'tp'), 0, 0, tiled=True)  22.9 us
    dot_general x1, matrix products, device_fn(): jnp.einsum('secm,emf->secf', tok_in, w_gate, preferred_element_type=jnp.f...  20.5 us
  transfers between devices with their start and end apart: 3, of which 2 were waited for; matrix products, arithmetic and copies ran while one was open for 18% of the time, Pallas kernels for 10%

profile of v1, /device:TPU:0, one launch (start us, length us, event | category | flops | bytes accessed | tf_op | source)
XLA Modules:
  0.0 563.6 jit_solution(4042048261206245212)
XLA Ops:
  6.5 0.0 copy-start
  6.5 0.0 all-gather.3.cloned.1.call-start
  6.5 0.7 all-gather.3.cloned.1.call-update
  7.3 0.0 all-gather.5.cloned.1.call-start
  7.3 0.7 all-gather.5.cloned.1.call-update
  8.0 4.5 constant_dynamic-slice_fusion
  12.5 3.7 copy.56
  16.2 2.0 copy.57
  18.2 0.0 copy-done
  18.2 1.1 constant_dynamic-slice_fusion.2
  19.3 0.8 copy.55
  20.1 75.9 %all-gather.3.cloned.1.call-done = bf16[4096,2048]{1,0:T(8,128)(2,1)} async-done(((bf16[512,2048]{1,0:T(8,128)(2,1)}), bf16[4096,2048]{1,0:T(8,128)(2,1)}) %all-gather.3.cloned.1.call-update) | async-done | bytes 16777232 | tf_op jit(solution)/shard_map/all_gather | solution.py:113
  96.1 19.1 %fusion.14 = bf16[4096,768]{0,1:T(8,128)(2,1)} fusion(bf16[4096,2048]{1,0:T(8,128)(2,1)} %all-gather.3.cloned.1.call-done, bf16[2048,256]{0,1:T(8,128)(2,1)} %bitcast.87, bf16[2048,256]{0,1:T(8,128)(2,1)} %bitcast.86, bf16[2048,256]{0,1:T(8,128)(2,1)S(1)} %bitcast.88), kind=kOutput, calls=%fused_computation.24 | convolution fusion | flops 12897484800 | bytes 26214400 | tf_op jit(solution)/shard_map/dot_general | solution.py:116
  115.1 11.1 %reshape.57 = bf16[2,4,2,256,768]{3,2,1,0,4:T(2,128)(2,1)} reshape(bf16[4096,768]{0,1:T(8,128)(2,1)} %fusion.14) | data formatting | bytes 12582912 | tf_op jit(solution)/shard_map/reshape | solution.py:95
  126.3 13.9 %fusion.33 = (bf16[2,4,1,256,768]{3,2,1,0,4:T(2,128)(2,1)}, bf16[2,4,1,256,768]{3,2,1,0,4:T(2,128)(2,1)}) fusion(bf16[2,4,2,256,768]{3,2,1,0,4:T(2,128)(2,1)} %reshape.57), kind=kLoop, calls=%fused_computation.48 | loop fusion | bytes 12582912 | tf_op jit(solution)/shard_map/slice | solution.py:96
  140.1 15.3 %copy.59 = bf16[2,4,1,256,768]{4,3,1,0,2:T(8,128)(2,1)} copy(bf16[2,4,1,256,768]{3,2,1,0,4:T(2,128)(2,1)} %get-tuple-element.9) | data formatting | bytes 6291456
  155.4 15.3 %copy.58 = bf16[2,4,1,256,768]{4,3,1,0,2:T(8,128)(2,1)} copy(bf16[2,4,1,256,768]{3,2,1,0,4:T(2,128)(2,1)} %get-tuple-element.8) | data formatting | bytes 6291456
  170.7 2.1 reverse_bitcast_fusion
  172.8 2.4 pad_maximum_fusion
  175.2 2.8 fusion.32
  178.1 55.1 %shard_map.100 = bf16[4096,256]{1,0:T(8,128)(2,1)} custom-call(bf16[4096,256]{1,0:T(8,128)(2,1)} %get-tuple-element.7.q_ref, bf16[4096,256]{1,0:T(8,128)(2,1)} %get-tuple-element.6.k_ref, bf16[4096,256]{1,0:T(8,128)(2,1)} %get-tuple-element.5.v_ref), custom_call_target="tpu_custom_call" | custom-call | flops 8589934592 | bytes 8388608 | tf_op jit(solution)/shard_map/pallas_call | solution.py:74
  233.2 1.7 fusion.34
  234.9 0.0 copy-start.5
  234.9 0.1 reverse_bitcast_fusion.1
  235.0 1.5 pad_maximum_fusion.1
  236.5 2.3 all-to-all-start
  238.8 0.0 copy-done.5
  238.8 0.1 copy.47
  239.0 0.2 eq.28
  239.2 0.6 fusion.29
  239.8 0.2 convert_element_type.52
  240.0 0.1 copy.48
  240.1 2.4 convert_reduce_fusion
  242.5 22.9 %all-to-all-done = bf16[8,512,256]{2,1,0:T(8,128)(2,1)S(1)} async-done(((bf16[8,512,256]{2,1,0:T(8,128)(2,1)}), bf16[8,512,256]{2,1,0:T(8,128)(2,1)S(1)}, u32[]{:S(2)}, u32[]{:S(2)}) %all-to-all-start) | async-done | bytes 2097184 | tf_op jit(solution)/shard_map/all_to_all | solution.py:120
  265.4 2.4 copy.46
  267.7 0.0 all-gather.5.cloned.1.call-done
  267.7 0.0 copy-start.2
  267.7 9.3 %add_convert_fusion.1 = bf16[512,2048]{1,0:T(8,128)(2,1)S(1)} fusion(bf16[512,2048]{1,0:T(8,128)(2,1)} %param.10, bf16[512,2048]{0,1:T(8,128)(2,1)} %bitcast.85, bf16[2048,2048]{1,0:T(8,128)(2,1)} %bitcast.89), kind=kOutput, calls=%fused_computation.28 | convolution fusion | flops 4298113024 | bytes 14680064 | tf_op jit(solution)/shard_map/dot_general | solution.py:122
  277.0 0.0 copy-done.2
  277.0 0.0 copy-start.3
  277.0 4.8 fusion.35
  281.8 0.0 copy-done.3
  281.9 96.3 %all_to_all.30 = bf16[8,256,2048]{2,1,0:T(8,128)(2,1)} all-to-all(bf16[8,256,2048]{2,1,0:T(8,128)(2,1)S(1)} %bitcast.80), channel_id=1, replica_groups=mesh['data'=1,'cp'=2,'tp'=4] {'cp','tp'}, dimensions={0} | all-to-all | bytes 16777216 | tf_op jit(solution)/shard_map/all_to_all | solution.py:134
  378.2 22.9 %fusion.2 = f32[8,8,32,1024]{3,2,1,0:T(8,128)} fusion(bf16[8,2048,1024]{2,1,0:T(8,128)(2,1)} %param.18, bf16[8,8,32,2048]{3,2,1,0:T(8,128)(2,1)} %bitcast.77), kind=kOutput, calls=%fused_computation.2 | convolution fusion | flops 8589934592 | bytes 50331648 | tf_op jit(solution)/shard_map/secm,emf->secf/dot_general | solution.py:137
  401.1 20.5 %fusion.6 = bf16[8,8,32,1024]{3,2,0,1:T(8,128)(2,1)} fusion(f32[8,8,32,1024]{3,2,1,0:T(8,128)} %fusion.2, bf16[8,2048,1024]{2,1,0:T(8,128)(2,1)} %param.17, bf16[8,8,32,2048]{3,2,1,0:T(8,128)(2,1)} %bitcast.78), kind=kOutput, calls=%fused_computation.7 | convolution fusion | flops 8602517504 | bytes 54525952 | tf_op jit(solution)/shard_map/secm,emf->secf/dot_general | solution.py:136
  421.5 18.3 %convert_bitcast_fusion = bf16[8,8,32,2048]{3,2,0,1:T(8,128)(2,1)} fusion(bf16[8,8,32,1024]{3,2,0,1:T(8,128)(2,1)} %fusion.6, bf16[8,1024,2048]{2,1,0:T(8,128)(2,1)} %param.19), kind=kOutput, calls=%fused_computation.14 | convolution fusion | flops 8594128896 | bytes 46137344 | tf_op jit(solution)/shard_map/secf,efm->secm/dot_general | solution.py:139
  439.8 8.3 %copy.51 = bf16[8,8,32,2048]{3,2,1,0:T(8,128)(2,1)} copy(bf16[8,8,32,2048]{3,2,0,1:T(8,128)(2,1)} %convert_bitcast_fusion) | data formatting | bytes 16777216 | tf_op jit(solution)/shard_map/convert_element_type | solution.py:139
  448.1 0.0 copy-start.6
  448.1 96.7 %all_to_all.31 = bf16[8,256,2048]{2,1,0:T(8,128)(2,1)S(1)} all-to-all(bf16[8,256,2048]{2,1,0:T(8,128)(2,1)} %bitcast.74), channel_id=1, replica_groups=mesh['data'=1,'cp'=2,'tp'=4] {'cp','tp'}, dimensions={0} | all-to-all | bytes 16777216 | tf_op jit(solution)/shard_map/all_to_all | solution.py:140
  544.8 0.0 copy-done.6
  544.8 0.0 copy-start.4
  544.8 0.0 copy-start.1
  544.8 9.4 %multiply_reduce_fusion = f32[512,2048]{1,0:T(8,128)S(1)} fusion(f32[512,2]{0,1:T(2,128)S(1)} %copy-done.6, bf16[2048,2048,1]{1,0,2:T(8,128)(2,1)S(1)} %bitcast.79, s32[512,2]{0,1:T(2,128)S(1)} %multiply_add_fusion), kind=kOutput, calls=%fused_computation.13 | convolution fusion | flops 8595177472 | bytes 12591104 | tf_op jit(solution)/shard_map/tkn,nm->tkm/dot_general | solution.py:141
  554.3 0.0 copy-done.4
  554.3 2.0 add_convert_fusion
  556.3 0.0 copy-done.1
  (2 shorter events, 0.0 us)
Async XLA Ops:
  6.5 11.7 %copy-start = (bf16[2048,4,128]{2,1,0:T(4,128)(2,1)S(1)}, bf16[2048,4,128]{2,1,0:T(4,128)(2,1)}, u32[]{:S(2)}) copy-start(bf16[2048,4,128]{2,1,0:T(4,128)(2,1)} %param.11) | copy-start | bytes 6291460
  6.5 89.6 %all-gather.3.cloned.1.call-start = ((), (), s32[]{:S(2)}) async-start(), calls=%async_computation.3 | async-start | bytes 18874368 | tf_op jit(solution)/shard_map/all_gather | solution.py:113
  7.3 260.5 %all-gather.5.cloned.1.call-start = ((), (), s32[]{:S(2)}) async-start(), calls=%async_computation.4 | async-start | bytes 10485760 | tf_op jit(solution)/shard_map/all_gather | solution.py:114
  234.9 4.0 copy-start.5
  236.5 28.9 %all-to-all-start = ((bf16[8,512,256]{2,1,0:T(8,128)(2,1)}), bf16[8,512,256]{2,1,0:T(8,128)(2,1)S(1)}, u32[]{:S(2)}, u32[]{:S(2)}) async-start(bf16[8,512,256]{2,1,0:T(8,128)(2,1)} %bitcast.82), calls=%async_computation | async-start | bytes 4194304 | tf_op jit(solution)/shard_map/all_to_all | solution.py:120
  267.7 9.3 %copy-start.2 = (bf16[512,2048]{1,0:T(8,128)(2,1)S(1)}, bf16[512,2048]{1,0:T(8,128)(2,1)}, u32[]{:S(2)}) copy-start(bf16[512,2048]{1,0:T(8,128)(2,1)} %convert_reduce_fusion) | copy-start | bytes 6291460
  277.0 4.8 copy-start.3
  448.1 96.7 %copy-start.6 = (f32[512,2]{0,1:T(2,128)S(1)}, f32[512,2]{0,1:T(2,128)}, u32[]{:S(2)}) copy-start(f32[512,2]{0,1:T(2,128)} %param.16) | copy-start | bytes 12292
  544.8 9.5 %copy-start.4 = (bf16[512,2048]{1,0:T(8,128)(2,1)S(1)}, bf16[512,2048]{1,0:T(8,128)(2,1)}, u32[]{:S(2)}) copy-start(bf16[512,2048]{1,0:T(8,128)(2,1)} %copy-done.3) | copy-start | bytes 6291460
  544.8 11.5 %copy-start.1 = (bf16[2048,4,128]{2,1,0:T(4,128)(2,1)S(1)}, bf16[2048,4,128]{2,1,0:T(4,128)(2,1)}, u32[]{:S(2)}) copy-start(bf16[2048,4,128]{2,1,0:T(4,128)(2,1)} %param.11) | copy-start | bytes 6291460
Sparse Core Ops, SparseCore 0:
  9.2 86.8 all-gather.2
  97.6 55.7 all-gather.4

commit v2 on v0

v2 whole, which is shorter than its diff:
```python
import functools
import math

import jax
import jax.numpy as jnp
from jax import lax
from jax.experimental import pallas as pl
from jax.experimental.pallas import tpu as pltpu
from jax.sharding import PartitionSpec as P

MESH = pl.DeviceIdType.MESH
MIB = 1024 * 1024
QB = 512


def lane_fold(s, op):
    out = s[:, :128]
    for g in range(1, s.shape[1] // 128):
        out = op(out, s[:, g * 128:(g + 1) * 128])
    return out


def attn_block(x_hbm, wqkv_ref, wo_hbm, h_ref, xbuf, qkv, s_ref, acc_ref, o_loc, o_cat, wo_buf,
               loc_sem, xs, xr, ws, wr, os_sem, or_sem, *, heads, head_dim):
    cp, tp = lax.axis_index('cp'), lax.axis_index('tp')
    xx, cc = tp // 2, tp % 2
    me = cp * 4 + tp
    ndev, rows, d_model = xbuf.shape
    half_rows = rows // 2
    quarter = half_rows // 2
    width = heads * head_dim
    seq = ndev * rows
    wrows = wo_hbm.shape[0]
    whalf, wquart = wrows // 2, wrows // 4

    def tp_of(dx, dc):
        return ((xx + dx) % 2) * 2 + (cc + dc) % 2

    def idx(dx, dy, dc):
        return ((cp + dy) % 2) * 4 + tp_of(dx, dc)

    def dev(dx, dy, dc):
        return {'cp': (cp + dy) % 2, 'tp': tp_of(dx, dc)}

    XN, YN, CN, DG = (1, 0, 0), (0, 1, 0), (0, 0, 1), (1, 1, 0)
    XC, YC, DC = (1, 0, 1), (0, 1, 1), (1, 1, 1)

    x_load = pltpu.make_async_copy(x_hbm, xbuf.at[me], loc_sem.at[0])
    wo_load = pltpu.make_async_copy(wo_hbm, wo_buf.at[pl.ds(tp * wrows, wrows)], loc_sem.at[1])
    x_load.start()
    wo_load.start()

    barrier = pltpu.get_barrier_semaphore()
    for k in range(1, ndev):
        peer = (me + k) % ndev
        pl.semaphore_signal(barrier, inc=1, device_id={'cp': peer // 4, 'tp': peer % 4}, device_id_type=MESH)
    pl.semaphore_wait(barrier, ndev - 1)

    def xcopy(slot, owner, row0, count, part, target):
        ref = xbuf.at[idx(*owner), pl.ds(row0, count)]
        return pltpu.make_async_remote_copy(src_ref=ref, dst_ref=ref, send_sem=xs.at[slot], recv_sem=xr.at[idx(*owner), part], device_id=dev(*target), device_id_type=MESH)

    sent = []

    def send(*args):
        copy = xcopy(*args)
        copy.start()
        sent.append(copy)

    def arrive(owner, row0, count, part):
        xcopy(0, owner, row0, count, part, CN).wait_recv()

    def wcopy(slot, shard, row0, count, sem, target):
        ref = wo_buf.at[pl.ds(shard * wrows + row0, count)]
        return pltpu.make_async_remote_copy(src_ref=ref, dst_ref=ref, send_sem=ws.at[slot], recv_sem=wr.at[sem], device_id=dev(*target), device_id_type=MESH)

    own = (0, 0, 0)
    x_load.wait()
    for half in range(2):
        send(0 + half, own, half * half_rows, half_rows, 2 * half, XN)
        send(2 + half, own, half * half_rows, half_rows, 2 * half, YN)
        send(4 + half, own, half * half_rows, half_rows, 2 * half, CN)
    wo_load.wait()
    w_own = wcopy(0, tp, 0, wrows, 0, CN)
    w_own.start()

    def project(owner, half):
        r, t = owner // 4, owner % 4
        seg = r + half * (3 - 2 * r)
        x = xbuf[owner, pl.ds(pl.multiple_of(half * half_rows, half_rows), half_rows), :]
        out = jnp.dot(x, wqkv_ref[...], preferred_element_type=jnp.float32).astype(jnp.bfloat16)
        qkv[pl.ds(pl.multiple_of((seg * 4 + t) * half_rows, half_rows), half_rows), :] = out

    def near(s, _):
        @pl.when(s == 2)
        def _():
            arrive(CN, 0, half_rows, 0)

        @pl.when(s == 3)
        def _():
            arrive(CN, half_rows, half_rows, 2)

        project(idx(0, 0, s // 2), s % 2)
        return 0

    lax.fori_loop(0, 4, near, 0)

    for half in range(2):
        base = half * half_rows
        arrive(XN, base, half_rows, 2 * half)
        send(6 + half, XN, base, half_rows, 2 * half, CN)
        send(12 + half, XN, base + quarter, quarter, 2 * half + 1, YN)
        arrive(YN, base, half_rows, 2 * half)
        send(8 + half, YN, base, half_rows, 2 * half, CN)
        send(10 + half, YN, base, quarter, 2 * half, XN)

        def mid(u, _):
            @pl.when(u == 2)
            def _():
                arrive(XC, base, half_rows, 2 * half)

            @pl.when(u == 3)
            def _():
                arrive(YC, base, half_rows, 2 * half)

            project(idx(1 - u % 2, u % 2, u // 2), half)
            return 0

        lax.fori_loop(0, 4, mid, 0)

    w_x = [wcopy(1 + k, tp, cp * whalf + k * wquart, wquart, 1 + k, XN) for k in range(2)]
    for copy in w_x:
        copy.start()

    for half in range(2):
        base = half * half_rows
        arrive(DG, base, quarter, 2 * half)
        arrive(DG, base + quarter, quarter, 2 * half + 1)
        send(14 + half, DG, base, half_rows, 2 * half, CN)

        def far(u, _):
            @pl.when(u == 1)
            def _():
                arrive(DC, base, half_rows, 2 * half)

            project(idx(1, 1, u), half)
            return 0

        lax.fori_loop(0, 2, far, 0)

    coef = (head_dim ** -0.5) * math.log2(math.e)
    my_col = (4 * tp + 2 * cp) * head_dim

    def o_place(b):
        seg, t = b // 4, b % 4
        half = seg // 2
        return seg + half * (3 - 2 * seg), t, half

    def o_remote(b):
        r, t, half = o_place(b)
        return pltpu.make_async_remote_copy(
            src_ref=o_loc.at[pl.ds(pl.multiple_of(b * half_rows, half_rows), half_rows)],
            dst_ref=o_cat.at[pl.ds(pl.multiple_of(half * half_rows, half_rows), half_rows), pl.ds(pl.multiple_of(my_col, width), width)],
            send_sem=os_sem.at[b], recv_sem=or_sem.at[me, half], device_id={'cp': r, 'tp': t}, device_id_type=MESH)

    def o_local(b):
        _, _, half = o_place(b)
        return pltpu.make_async_copy(
            o_loc.at[pl.ds(pl.multiple_of(b * half_rows, half_rows), half_rows)],
            o_cat.at[pl.ds(pl.multiple_of(half * half_rows, half_rows), half_rows), pl.ds(pl.multiple_of(my_col, width), width)],
            os_sem.at[b])

    def o_send(i):
        for part in range(QB // half_rows):
            b = i * (QB // half_rows) + part
            r, t, _ = o_place(b)

            @pl.when(r * 4 + t != me)
            def _():
                o_remote(b).start()

            @pl.when(r * 4 + t == me)
            def _():
                o_local(b).start()

    peer_t = tp_of(1, 0)
    peer_c = tp_of(1, 1)

    def w_pass(k):
        wcopy(1, peer_t, cp * whalf + k * wquart, wquart, 1 + k, CN).wait_recv()
        wcopy(3 + k, peer_t, cp * whalf + k * wquart, wquart, 3 + k, YN).start()
        wcopy(5 + k, peer_t, cp * whalf + k * wquart, wquart, 5 + k, CN).start()

    def w_last(k):
        wcopy(1, peer_t, (1 - cp) * whalf + k * wquart, wquart, 3 + k, CN).wait_recv()
        wcopy(7 + k, peer_t, (1 - cp) * whalf + k * wquart, wquart, 7 + k, CN).start()

    blocks = seq // QB

    def q_step(i, _):
        @pl.when(i == blocks - 3)
        def _():
            w_pass(0)

        @pl.when(i == blocks - 2)
        def _():
            w_pass(1)

        @pl.when(i == blocks - 1)
        def _():
            w_last(0)

        q_rows = pl.ds(pl.multiple_of(i * QB, QB), QB)

        def cols(kind, h):
            return slice(kind * width + h * head_dim, kind * width + (h + 1) * head_dim)

        def scores(h, j):
            k = qkv[pl.ds(pl.multiple_of(j * QB, QB), QB), cols(1, h)]
            return lax.dot_general(qkv[q_rows, cols(0, h)], k, (((1,), (1,)), ((), ())), preferred_element_type=jnp.float32)

        def pass1(j, ms):
            out = []
            for h in range(heads):
                s = scores(h, j)
                s_ref[h, :, pl.ds(pl.multiple_of(j * QB, QB), QB)] = s
                out.append(jnp.maximum(ms[h], lane_fold(s, jnp.maximum)))
            return tuple(out)

        ms = lax.fori_loop(0, i, pass1, tuple(jnp.full((QB, 128), -jnp.inf, jnp.float32) for _ in range(heads)))
        keep = lax.broadcasted_iota(jnp.int32, (QB, QB), 1) <= lax.broadcasted_iota(jnp.int32, (QB, QB), 0)
        tops = []
        for h in range(heads):
            s = jnp.where(keep, scores(h, i), -jnp.inf)
            s_ref[h, :, pl.ds(pl.multiple_of(i * QB, QB), QB)] = s
            tops.append(jnp.max(jnp.maximum(ms[h], lane_fold(s, jnp.maximum)), axis=1, keepdims=True))
        acc_ref[...] = jnp.zeros_like(acc_ref)

        def pass2(j, ls):
            out = []
            for h in range(heads):
                e = jnp.exp2((s_ref[h, :, pl.ds(pl.multiple_of(j * QB, QB), QB)] - tops[h]) * coef)
                v = qkv[pl.ds(pl.multiple_of(j * QB, QB), QB), cols(2, h)]
                acc_ref[h] += jnp.dot(e.astype(jnp.bfloat16), v, preferred_element_type=jnp.float32)
                out.append(ls[h] + lane_fold(e, jnp.add))
            return tuple(out)

        ls = lax.fori_loop(0, i + 1, pass2, tuple(jnp.zeros((QB, 128), jnp.float32) for _ in range(heads)))
        for h in range(heads):
            total = jnp.sum(ls[h], axis=1, keepdims=True)
            o_loc[q_rows, h * head_dim:(h + 1) * head_dim] = (acc_ref[h] / total).astype(jnp.bfloat16)
        o_send(i)
        return 0

    lax.fori_loop(0, blocks, q_step, 0)

    w_last(1)
    wcopy(1, tp_of(0, 1), 0, wrows, 0, CN).wait_recv()
    for k in range(2):
        wcopy(1, peer_c, cp * whalf + k * wquart, wquart, 5 + k, CN).wait_recv()
        wcopy(1, peer_c, (1 - cp) * whalf + k * wquart, wquart, 7 + k, CN).wait_recv()
    for k in range(1, ndev):
        src = (me + k) % ndev
        col = (4 * (src % 4) + 2 * (src // 4)) * head_dim
        for half in range(2):
            ref = o_cat.at[pl.ds(half * half_rows, half_rows), pl.ds(pl.multiple_of(col, width), width)]
            pltpu.make_async_remote_copy(src_ref=ref, dst_ref=ref, send_sem=os_sem.at[0], recv_sem=or_sem.at[src, half], device_id=dev(0, 0, 1), device_id_type=MESH).wait_recv()

    def drain(b, _):
        r, t, _half = o_place(b)

        @pl.when(r * 4 + t != me)
        def _():
            o_remote(b).wait_send()

        @pl.when(r * 4 + t == me)
        def _():
            o_local(b).wait()

        return 0

    lax.fori_loop(0, seq // half_rows, drain, 0)

    tile = 256

    def out_step(n, _):
        c = pl.ds(pl.multiple_of(n * tile, tile), tile)
        a = jnp.dot(o_cat[...], wo_buf[:, c], preferred_element_type=jnp.float32)
        h_ref[:, c] = (xbuf[me, :, c].astype(jnp.float32) + a).astype(jnp.bfloat16)
        return 0

    lax.fori_loop(0, d_model // tile, out_step, 0)

    for copy in sent:
        copy.wait_send()
    w_own.wait_send()
    for copy in w_x:
        copy.wait_send()
    for k in range(2):
        wcopy(3 + k, peer_t, cp * whalf + k * wquart, wquart, 3 + k, YN).wait_send()
        wcopy(5 + k, peer_t, cp * whalf + k * wquart, wquart, 5 + k, CN).wait_send()
        wcopy(7 + k, peer_t, (1 - cp) * whalf + k * wquart, wquart, 7 + k, CN).wait_send()


def attention_block(x_blk, w_qkv, w_o, heads, head_dim, ndev):
    rows, d_model = x_blk.shape
    seq = rows * ndev
    width = heads * head_dim
    vm = pl.BlockSpec(memory_space=pltpu.VMEM)
    hbm = pl.BlockSpec(memory_space=pl.ANY)
    bf16, f32 = jnp.bfloat16, jnp.float32
    dma = pltpu.SemaphoreType.DMA
    return pl.pallas_call(
        functools.partial(attn_block, heads=heads, head_dim=head_dim),
        name='attn_block',
        out_shape=jax.ShapeDtypeStruct((rows, d_model), bf16),
        in_specs=[hbm, vm, hbm],
        out_specs=vm,
        scratch_shapes=[
            pltpu.VMEM((ndev, rows, d_model), bf16), pltpu.VMEM((seq, 3 * width), bf16),
            pltpu.VMEM((heads, QB, seq), f32), pltpu.VMEM((heads, QB, head_dim), f32),
            pltpu.VMEM((seq, width), bf16), pltpu.VMEM((rows, ndev * width), bf16),
            pltpu.VMEM((ndev * width, d_model), bf16),
            dma((2,)), dma((16,)), dma((ndev, 4)), dma((9,)), dma((9,)), dma((16,)), dma((ndev, 2)),
        ],
        compiler_params=pltpu.CompilerParams(collective_id=0, has_side_effects=True, vmem_limit_bytes=63 * MIB),
        cost_estimate=pl.CostEstimate(flops=2 * seq * d_model * width * 3 + 4 * seq * seq * width, bytes_accessed=16 * MIB, transcendentals=0),
    )(x_blk, w_qkv, w_o)


def solution(mesh):
    cp_size = mesh.shape['cp']
    tp_size = mesh.shape['tp']
    num_devs = cp_size * tp_size
    row_spec = P(('data', 'cp', 'tp'), None)
    head_spec = P(None, 'tp', None)
    wo_spec = P('tp', None, None)
    expert_spec = P(('cp', 'tp'), None, None)

    def device_fn(x_blk, w_q, w_k, w_v, w_o, idx_blk, gate_blk, w_gate, w_up, w_down):
        tok_dev, d_model = x_blk.shape
        heads_tp, head_dim = w_q.shape[1], w_q.shape[2]
        heads = heads_tp // cp_size
        width = heads * head_dim
        exp_local = w_gate.shape[0]
        num_exp = exp_local * num_devs
        capacity = 4 * tok_dev // num_exp
        cp_rank = lax.axis_index('cp')

        w_qkv = jnp.concatenate([lax.dynamic_slice_in_dim(w, cp_rank * heads, heads, 1).reshape(d_model, width) for w in (w_q, w_k, w_v)], axis=1)
        hidden = attention_block(x_blk, w_qkv, w_o.reshape(-1, d_model), heads, head_dim, num_devs)

        flat_ids = idx_blk.reshape(-1)
        num_flat = flat_ids.shape[0]
        onehot = (flat_ids[:, None] == jnp.arange(num_exp)[None, :])
        before = (jnp.arange(num_flat)[:, None] > jnp.arange(num_flat)[None, :]).astype(jnp.bfloat16)
        ranks = jnp.dot(before, onehot.astype(jnp.bfloat16), preferred_element_type=jnp.float32)
        slot_pos = jnp.sum(jnp.where(onehot, ranks, 0.0), axis=1).astype(jnp.int32)
        slot_ids = (flat_ids * capacity + slot_pos).reshape(tok_dev, 2)
        select = (slot_ids[:, :, None] == jnp.arange(num_exp * capacity)[None, None, :]).astype(jnp.bfloat16)
        send_buf = jnp.einsum('tkn,tm->nm', select, hidden, preferred_element_type=jnp.float32).astype(jnp.bfloat16)
        recv_buf = lax.all_to_all(send_buf, ('cp', 'tp'), 0, 0, tiled=True)
        tok_in = recv_buf.reshape(num_devs, exp_local, capacity, -1)
        gate_pre = jnp.einsum('secm,emf->secf', tok_in, w_gate, preferred_element_type=jnp.float32)
        up_pre = jnp.einsum('secm,emf->secf', tok_in, w_up, preferred_element_type=jnp.float32)
        hid_act = (jax.nn.silu(gate_pre) * up_pre).astype(jnp.bfloat16)
        exp_out = jnp.einsum('secf,efm->secm', hid_act, w_down, preferred_element_type=jnp.float32).astype(jnp.bfloat16)
        back_buf = lax.all_to_all(exp_out.reshape(num_devs * exp_local * capacity, -1), ('cp', 'tp'), 0, 0, tiled=True)
        picked = jnp.einsum('tkn,nm->tkm', select, back_buf, preferred_element_type=jnp.float32)
        moe_out = jnp.sum(gate_blk[:, :, None] * picked, axis=1)
        return (hidden.astype(jnp.float32) + moe_out).astype(jnp.bfloat16)

    return jax.shard_map(device_fn, mesh=mesh, in_specs=(row_spec, head_spec, head_spec, head_spec, wo_spec, row_spec, row_spec, expert_spec, expert_spec, expert_spec), out_specs=row_spec, check_vma=False)
```

time: 706 us -> 450 us (0.64); the launches traced: 698 us -> 450 us
  waiting for transfers between devices: 187 us -> 0 us
  Pallas kernels: 0 us -> 144 us
  matrix products: 219 us -> 78.4 us
  other arithmetic: 74.7 us -> 8.05 us
  between operations: 13.7 us -> 0.12 us
  local copies, waits for them, and re-layouts: 10.1 us -> 21.2 us
    pallas_call x0 -> x1, Pallas kernels: none -> 144 us  [attention_block(): pl.pallas_call(functools.partial(attn_block, heads=heads, head_dim=head_d...]
    dot_general x6 -> x1, matrix products: 140 us -> 0.6 us  [device_fn(): jnp.dot(before, onehot.astype(jnp.bfloat16), preferred_element_type=jnp.f...]
    reduce_scatter x1 -> x0, waiting for transfers between devices: 96.5 us -> none  [device_fn(): attn_out = lax.psum_scatter(part_sum, 'tp', scatter_dimension=0, tiled=True)]
    all_gather x3 -> x0, waiting for transfers between devices: 89.5 us -> none  [the longest x1 60.1 us: device_fn(): x_rows = lax.all_gather(x_blk, 'tp', axis=0, tiled=True)]
    reduce_sum x2 -> x0, other arithmetic: 43.9 us -> none  [the longest x1 43.8 us: device_fn(): jnp.sum(exp_scores, axis=-1, keepdims=True)]
    another operation x3 -> x0, other arithmetic: 18.2 us -> none
    le x1 -> x0, other arithmetic: 7.6 us -> none  [device_fn(): pos_k[None, None, None, :] <= pos_q[None, None, :, None]]
  transfers between devices with their start and end apart: 4 -> 0, of which waited for: 3 -> 0; matrix products, arithmetic and copies ran while one was open for 20% -> 0% of each run, Pallas kernels for 0% -> 0%
where the time goes in v2:
time: 450 us
  blocking collectives  198 us (44%)
  Pallas kernels  144 us (32%)
  matrix products  78.4 us (17%)
  local copies, waits for them, and re-layouts  21.2 us (5%)
  other arithmetic  8.05 us (2%)
    pallas_call x1, Pallas kernels, attention_block(): pl.pallas_call(functools.partial(attn_block, heads=heads, head_dim=head_d...  144 us
    all_to_all x1, blocking collectives, device_fn(): recv_buf = lax.all_to_all(send_buf, ('cp', 'tp'), 0, 0, tiled=True)  102 us
    all_to_all x1, blocking collectives, device_fn(): lax.all_to_all(exp_out.reshape(num_devs * exp_local * capacity, -1), ('cp...  96.5 us
    dot_general x1, matrix products, device_fn(): jnp.einsum('secm,emf->secf', tok_in, w_up, preferred_element_type=jnp.flo...  22.8 us
    dot_general x1, matrix products, device_fn(): jnp.einsum('secm,emf->secf', tok_in, w_gate, preferred_element_type=jnp.f...  20.4 us
    dot_general x1, matrix products, device_fn(): jnp.einsum('secf,efm->secm', hid_act, w_down, preferred_element_type=jnp....  18.3 us
    dot_general x1, matrix products, device_fn(): jnp.einsum('tkn,nm->tkm', select, back_buf, preferred_element_type=jnp.fl...  9.45 us

profile of v2, /device:TPU:0, one launch (start us, length us, event | category | flops | bytes accessed | tf_op | source)
XLA Modules:
  0.0 449.6 jit_solution(7933596164411546292)
XLA Ops:
  0.0 0.8 copy.29
  0.8 0.2 eq.28
  1.0 0.6 fusion.23
  1.6 0.2 convert_element_type.36
  1.8 0.1 copy.30
  1.9 0.7 multiply_add_fusion
  2.6 2.3 constant_dynamic-slice_fusion.2
  5.0 0.8 copy.37
  5.8 1.3 copy.26
  7.1 3.7 constant_dynamic-slice_fusion
  10.9 0.8 copy.39
  11.7 1.3 copy.28
  13.0 0.8 copy.38
  13.8 0.5 copy.27
  14.4 2.3 convert_reduce_fusion
  16.7 3.0 pad_maximum_fusion.wqkv_ref
  19.7 143.5 %attn_block.1 = bf16[512,2048]{1,0:T(8,128)(2,1)} custom-call(bf16[512,2048]{1,0:T(8,128)(2,1)} %x_hbm.1, bf16[2048,768]{1,0:T(8,128)(2,1)} %pad_maximum_fusion.wqkv_ref, bf16[512,2048]{1,0:T(8,128)(2,1)} %bitcast.60), custom_call_target="tpu_custom_call" | custom-call | flops 30064771072 | bytes 16777216 | tf_op jit(solution)/shard_map/attn_block/pallas_call | solution.py:313
  163.2 6.8 %fusion.25 = bf16[2048,2048]{1,0:T(8,128)(2,1)S(1)} fusion(bf16[512,2048]{1,0:T(8,128)(2,1)} %convert_reduce_fusion, bf16[512,2048]{1,0:T(8,128)(2,1)} %attn_block.1), kind=kOutput, calls=%fused_computation.35 | convolution fusion | flops 4294967296 | bytes 12582912 | tf_op jit(solution)/shard_map/tkn,tm->nm/dot_general | solution.py:361
  170.0 101.8 %all_to_all.21 = bf16[8,256,2048]{2,1,0:T(8,128)(2,1)} all-to-all(bf16[8,256,2048]{2,1,0:T(8,128)(2,1)S(1)} %bitcast.56), channel_id=1, replica_groups=mesh['data'=1,'cp'=2,'tp'=4] {'cp','tp'}, dimensions={0} | all-to-all | bytes 16777216 | tf_op jit(solution)/shard_map/all_to_all | solution.py:362
  271.9 22.8 %fusion.2 = f32[8,8,32,1024]{3,2,1,0:T(8,128)} fusion(bf16[8,2048,1024]{2,1,0:T(8,128)(2,1)} %param.18, bf16[8,8,32,2048]{3,2,1,0:T(8,128)(2,1)} %bitcast.53), kind=kOutput, calls=%fused_computation.2 | convolution fusion | flops 8589934592 | bytes 50331648 | tf_op jit(solution)/shard_map/secm,emf->secf/dot_general | solution.py:365
  294.7 20.4 %fusion.6 = bf16[8,8,32,1024]{3,2,0,1:T(8,128)(2,1)} fusion(f32[8,8,32,1024]{3,2,1,0:T(8,128)} %fusion.2, bf16[8,2048,1024]{2,1,0:T(8,128)(2,1)} %param.17, bf16[8,8,32,2048]{3,2,1,0:T(8,128)(2,1)} %bitcast.54), kind=kOutput, calls=%fused_computation.7 | convolution fusion | flops 8602517504 | bytes 54525952 | tf_op jit(solution)/shard_map/secm,emf->secf/dot_general | solution.py:364
  315.1 18.3 %convert_bitcast_fusion = bf16[8,8,32,2048]{3,2,0,1:T(8,128)(2,1)} fusion(bf16[8,8,32,1024]{3,2,0,1:T(8,128)(2,1)} %fusion.6, bf16[8,1024,2048]{2,1,0:T(8,128)(2,1)} %param.19), kind=kOutput, calls=%fused_computation.14 | convolution fusion | flops 8594128896 | bytes 46137344 | tf_op jit(solution)/shard_map/secf,efm->secm/dot_general | solution.py:367
  333.4 8.3 %copy.33 = bf16[8,8,32,2048]{3,2,1,0:T(8,128)(2,1)} copy(bf16[8,8,32,2048]{3,2,0,1:T(8,128)(2,1)} %convert_bitcast_fusion) | data formatting | bytes 16777216 | tf_op jit(solution)/shard_map/convert_element_type | solution.py:367
  341.6 0.0 copy-start.1
  341.6 96.5 %all_to_all.22 = bf16[8,256,2048]{2,1,0:T(8,128)(2,1)S(1)} all-to-all(bf16[8,256,2048]{2,1,0:T(8,128)(2,1)} %bitcast.52), channel_id=1, replica_groups=mesh['data'=1,'cp'=2,'tp'=4] {'cp','tp'}, dimensions={0} | all-to-all | bytes 16777216 | tf_op jit(solution)/shard_map/all_to_all | solution.py:368
  438.1 0.0 copy-done.1
  438.1 0.0 copy-start
  438.1 9.4 %multiply_reduce_fusion = f32[512,2048]{1,0:T(8,128)S(1)} fusion(f32[512,2]{0,1:T(2,128)S(1)} %copy-done.1, bf16[2048,2048,1]{1,0,2:T(8,128)(2,1)S(1)} %bitcast.55, s32[512,2]{0,1:T(2,128)S(1)} %multiply_add_fusion), kind=kOutput, calls=%fused_computation.13 | convolution fusion | flops 8595177472 | bytes 12591104 | tf_op jit(solution)/shard_map/tkn,nm->tkm/dot_general | solution.py:369
  447.6 0.0 copy-done
  447.6 2.0 add_convert_fusion
  (1 shorter events, 0.0 us)
Async XLA Ops:
  341.6 96.5 %copy-start.1 = (f32[512,2]{0,1:T(2,128)S(1)}, f32[512,2]{0,1:T(2,128)}, u32[]{:S(2)}) copy-start(f32[512,2]{0,1:T(2,128)} %param.16) | copy-start | bytes 12292
  438.1 9.5 %copy-start = (bf16[512,2048]{1,0:T(8,128)(2,1)S(1)}, bf16[512,2048]{1,0:T(8,128)(2,1)}, u32[]{:S(2)}) copy-start(bf16[512,2048]{1,0:T(8,128)(2,1)} %attn_block.1) | copy-start | bytes 6291460

commit v3 on v2

--- a/solution.py
+++ b/solution.py
@@ -20,8 +20,8 @@
     return out
 
 
-def attn_block(x_hbm, wqkv_ref, wo_hbm, h_ref, xbuf, qkv, s_ref, acc_ref, o_loc, o_cat, wo_buf,
-               loc_sem, xs, xr, ws, wr, os_sem, or_sem, *, heads, head_dim):
+def attn_block(x_hbm, wqkv_ref, wo_hbm, flag_ref, h_ref, any_ref, xbuf, qkv, s_ref, acc_ref, o_loc, o_cat, wo_buf,
+               flags, loc_sem, xs, xr, ws, wr, os_sem, or_sem, fs, fr, *, heads, head_dim):
     cp, tp = lax.axis_index('cp'), lax.axis_index('tp')
     xx, cc = tp // 2, tp % 2
     me = cp * 4 + tp
@@ -73,6 +73,13 @@
     def wcopy(slot, shard, row0, count, sem, target):
         ref = wo_buf.at[pl.ds(shard * wrows + row0, count)]
         return pltpu.make_async_remote_copy(src_ref=ref, dst_ref=ref, send_sem=ws.at[slot], recv_sem=wr.at[sem], device_id=dev(*target), device_id_type=MESH)
+
+    def flag_copy(j):
+        peer = (me + j) % ndev
+        return pltpu.make_async_remote_copy(src_ref=flag_ref, dst_ref=flags.at[me], send_sem=fs.at[j], recv_sem=fr.at[me], device_id={'cp': peer // 4, 'tp': peer % 4}, device_id_type=MESH)
+
+    for j in range(1, ndev):
+        flag_copy(j).start()
 
     own = (0, 0, 0)
     x_load.wait()
@@ -291,6 +298,14 @@
 
     lax.fori_loop(0, d_model // tile, out_step, 0)
 
+    most = flag_ref[...]
+    for j in range(1, ndev):
+        peer = (me + j) % ndev
+        pltpu.make_async_remote_copy(src_ref=flag_ref, dst_ref=flags.at[peer], send_sem=fs.at[j], recv_sem=fr.at[peer], device_id=dev(0, 0, 1), device_id_type=MESH).wait_recv()
+        most = jnp.maximum(most, flags[peer])
+        flag_copy(j).wait_send()
+    any_ref[...] = most
+
     for copy in sent:
         copy.wait_send()
     w_own.wait_send()
@@ -302,7 +317,7 @@
         wcopy(7 + k, peer_t, (1 - cp) * whalf + k * wquart, wquart, 7 + k, CN).wait_send()
 
 
-def attention_block(x_blk, w_qkv, w_o, heads, head_dim, ndev):
+def attention_block(x_blk, w_qkv, w_o, flag, heads, head_dim, ndev):
     rows, d_model = x_blk.shape
     seq = rows * ndev
     width = heads * head_dim
@@ -313,19 +328,259 @@
     return pl.pallas_call(
         functools.partial(attn_block, heads=heads, head_dim=head_dim),
         name='attn_block',
-        out_shape=jax.ShapeDtypeStruct((rows, d_model), bf16),
-        in_specs=[hbm, vm, hbm],
-        out_specs=vm,
+        out_shape=(jax.ShapeDtypeStruct((rows, d_model), bf16), jax.ShapeDtypeStruct(flag.shape, f32)),
+        in_specs=[hbm, vm, hbm, vm],
+        out_specs=(vm, vm),
         scratch_shapes=[
             pltpu.VMEM((ndev, rows, d_model), bf16), pltpu.VMEM((seq, 3 * width), bf16),
             pltpu.VMEM((heads, QB, seq), f32), pltpu.VMEM((heads, QB, head_dim), f32),
             pltpu.VMEM((seq, width), bf16), pltpu.VMEM((rows, ndev * width), bf16),
             pltpu.VMEM((ndev * width, d_model), bf16),
-            dma((2,)), dma((16,)), dma((ndev, 4)), dma((9,)), dma((9,)), dma((16,)), dma((ndev, 2)),
+            pltpu.VMEM((ndev,) + flag.shape, f32),
+            dma((2,)), dma((16,)), dma((ndev, 4)), dma((9,)), dma((9,)), dma((16,)), dma((ndev, 2)), dma((ndev,)), dma((ndev,)),
         ],
         compiler_params=pltpu.CompilerParams(collective_id=0, has_side_effects=True, vmem_limit_bytes=63 * MIB),
         cost_estimate=pl.CostEstimate(flops=2 * seq * d_model * width * 3 + 4 * seq * seq * width, bytes_accessed=16 * MIB, transcendentals=0),
-    )(x_blk, w_qkv, w_o)
+    )(x_blk, w_qkv, w_o, flag)
+
+
+def moe_block(h_ref, rl_ref, rc_ref, g_ref, meta_ref, wg_hbm, wu_hbm, wd_hbm, y_ref, send, recv, zbuf, ret,
+              meta_in, xs, zacc, acc, wg, wu, wd, ds, dr, rs, rr, ls, ms, mr, wsem, *, main, spill):
+    cp, tp = lax.axis_index('cp'), lax.axis_index('tp')
+    me = cp * 4 + tp
+    chunks, ndev, crow, d_model = send.shape
+    rows_all = ndev * crow
+    toks = h_ref.shape[0]
+    experts = wg_hbm.shape[0]
+    slots, _, ff_half = wg.shape
+    first = 1 if spill else 0
+    steps = 2 * experts
+    tile = 512
+    f32, bf16 = jnp.float32, jnp.bfloat16
+
+    def weights(n):
+        e, f, slot = n // 2, n % 2, n % slots
+        fcols = pl.ds(pl.multiple_of(f * ff_half, ff_half), ff_half)
+        return (pltpu.make_async_copy(wg_hbm.at[e, :, fcols], wg.at[slot], wsem.at[slot, 0]),
+                pltpu.make_async_copy(wu_hbm.at[e, :, fcols], wu.at[slot], wsem.at[slot, 1]),
+                pltpu.make_async_copy(wd_hbm.at[e, fcols, :], wd.at[slot], wsem.at[slot, 2]))
+
+    def fetch(n):
+        for copy in weights(n):
+            copy.start()
+
+    for n in range(slots - 1):
+        fetch(n)
+
+    def peer_of(j):
+        return (me + j) % ndev
+
+    def dev(p):
+        return {'cp': p // 4, 'tp': p % 4}
+
+    barrier = pltpu.get_barrier_semaphore()
+    for j in range(1, ndev):
+        pl.semaphore_signal(barrier, inc=1, device_id=dev(peer_of(j)), device_id_type=MESH)
+    pl.semaphore_wait(barrier, ndev - 1)
+
+    def meta_copy(j):
+        return pltpu.make_async_remote_copy(src_ref=meta_ref.at[peer_of(j)], dst_ref=meta_in.at[me], send_sem=ms.at[j], recv_sem=mr.at[me], device_id=dev(peer_of(j)), device_id_type=MESH)
+
+    if spill:
+        for j in range(1, ndev):
+            meta_copy(j).start()
+
+    def exchange(src, dst, ssem, rsem, k):
+        def copy(j):
+            return pltpu.make_async_remote_copy(src_ref=src.at[k, peer_of(j)], dst_ref=dst.at[k, me], send_sem=ssem.at[k, j], recv_sem=rsem.at[k, me], device_id=dev(peer_of(j)), device_id_type=MESH)
+
+        local = pltpu.make_async_copy(src.at[k, me], dst.at[k, me], ssem.at[k, 0])
+        return copy, local
+
+    def begin(src, dst, ssem, rsem, k):
+        copy, local = exchange(src, dst, ssem, rsem, k)
+        local.start()
+        for j in range(1, ndev):
+            copy(j).start()
+
+    def arrived(src, dst, ssem, rsem, k):
+        for j in range(1, ndev):
+            pltpu.make_async_remote_copy(src_ref=src.at[k, peer_of(j)], dst_ref=dst.at[k, peer_of(j)], send_sem=ssem.at[k, j], recv_sem=rsem.at[k, peer_of(j)], device_id=dev(peer_of(j)), device_id_type=MESH).wait_recv()
+        exchange(src, dst, ssem, rsem, k)[1].wait()
+
+    def left(src, dst, ssem, rsem, k):
+        copy, _ = exchange(src, dst, ssem, rsem, k)
+        for j in range(1, ndev):
+            copy(j).wait_send()
+
+    out_way = (send, recv, ds, dr)
+    back_way = (zbuf, ret, rs, rr)
+
+    def pack(k, _):
+        ids = lax.broadcasted_iota(jnp.int32, (rows_all, toks), 0) + k * rows_all
+        pick = ((ids == rl_ref[0:1, :]) | (ids == rl_ref[1:2, :])).astype(f32).astype(bf16)
+
+        def cols(n, _):
+            c = pl.ds(pl.multiple_of(n * tile, tile), tile)
+            rows = jnp.dot(pick, h_ref[:, c], preferred_element_type=f32).astype(bf16)
+            send[k, :, :, c] = rows.reshape(ndev, crow, tile)
+            return 0
+
+        lax.fori_loop(0, d_model // tile, cols, 0)
+
+        @pl.when(k > 0)
+        def _():
+            begin(*out_way, k - 1)
+
+        return 0
+
+    lax.fori_loop(0, chunks, pack, 0)
+    begin(*out_way, chunks - 1)
+
+    if spill:
+        for j in range(1, ndev):
+            p = peer_of(j)
+            pltpu.make_async_remote_copy(src_ref=meta_ref.at[p], dst_ref=meta_in.at[p], send_sem=ms.at[j], recv_sem=mr.at[p], device_id=dev(p), device_id_type=MESH).wait_recv()
+        arrived(*out_way, 0)
+        total = meta_ref[me]
+        for j in range(1, ndev):
+            total = total + meta_in[peer_of(j)]
+        code = total[0:1, :].astype(jnp.int32) - 1
+        lane = lax.broadcasted_iota(jnp.int32, code.shape, 1)
+        place = (lane // crow) * main + (code & (main - 1))
+        owner = code // main
+        zbuf[0] = jnp.zeros((ndev, crow, d_model), bf16)
+    body = ndev * main
+
+    def expert(e, _):
+        k = first + e // 2
+        part = pl.ds(pl.multiple_of((e % 2) * main, main), main)
+
+        @pl.when(e % 2 == 0)
+        def _():
+            arrived(*out_way, k)
+
+        xs[0:body, :] = recv[k, :, part, :].reshape(body, d_model)
+        if spill:
+            slot_id = lax.broadcasted_iota(jnp.int32, (body, rows_all), 0)
+            pick = ((slot_id == place) & (owner == e)).astype(f32).astype(bf16)
+
+            def gather(n, _):
+                c = pl.ds(pl.multiple_of(n * tile, tile), tile)
+                xs[body:2 * body, c] = jnp.dot(pick, recv[0, :, :, c].reshape(rows_all, tile), preferred_element_type=f32).astype(bf16)
+                return 0
+
+            lax.fori_loop(0, d_model // tile, gather, 0)
+
+        for f in range(2):
+            n = 2 * e + f
+            slot = n % slots
+            for copy in weights(n):
+                copy.wait()
+
+            @pl.when(n + slots - 1 < steps)
+            def _():
+                fetch(n + slots - 1)
+
+            x = xs[...]
+            gate = jnp.dot(x, wg[slot], preferred_element_type=f32)
+            up = jnp.dot(x, wu[slot], preferred_element_type=f32)
+            u = (gate * jax.nn.sigmoid(gate) * up).astype(bf16)
+
+            def down(n, _):
+                c = pl.ds(pl.multiple_of(n * tile, tile), tile)
+                z = jnp.dot(u, wd[slot, :, c], preferred_element_type=f32)
+                if f == 0:
+                    zacc[:, c] = z
+                else:
+                    z = (zacc[:, c] + z).astype(bf16)
+                    zbuf[k, :, part, c] = z[0:body].reshape(ndev, main, tile)
+                    if spill:
+                        spread = lax.dot_general(pick, z[body:], (((0,), (0,)), ((), ())), preferred_element_type=f32)
+                        zbuf[0, :, :, c] = zbuf[0, :, :, c] + spread.astype(bf16).reshape(ndev, crow, tile)
+                return 0
+
+            lax.fori_loop(0, d_model // tile, down, 0)
+            if f == 0:
+                @pl.when((e % 2 == 0) & (e > 0))
+                def _():
+                    begin(*back_way, k - 1)
+
+        return 0
+
+    lax.fori_loop(0, experts, expert, 0)
+    begin(*back_way, chunks - 1)
+    if spill:
+        begin(*back_way, 0)
+
+    acc[...] = jnp.zeros_like(acc)
+
+    def combine(kk, _):
+        k = (kk + first) % chunks
+        arrived(*back_way, k)
+        ids = lax.broadcasted_iota(jnp.int32, (toks, rows_all), 1) + k * rows_all
+        pick0 = (ids == rc_ref[:, 0:1]).astype(f32).astype(bf16)
+        pick1 = (ids == rc_ref[:, 1:2]).astype(f32).astype(bf16)
+
+        def cols(n, _):
+            c = pl.ds(pl.multiple_of(n * tile, tile), tile)
+            z = ret[k, :, :, c].reshape(rows_all, tile)
+            z0 = jnp.dot(pick0, z, preferred_element_type=f32)
+            z1 = jnp.dot(pick1, z, preferred_element_type=f32)
+            acc[:, c] += g_ref[:, 0:1] * z0 + g_ref[:, 1:2] * z1
+            return 0
+
+        lax.fori_loop(0, d_model // tile, cols, 0)
+        return 0
+
+    lax.fori_loop(0, chunks, combine, 0)
+
+    def finish(n, _):
+        c = pl.ds(pl.multiple_of(n * tile, tile), tile)
+        y_ref[:, c] = (h_ref[:, c].astype(f32) + acc[:, c]).astype(bf16)
+        return 0
+
+    lax.fori_loop(0, d_model // tile, finish, 0)
+
+    def drain(k, _):
+        left(*out_way, k)
+        left(*back_way, k)
+        return 0
+
+    lax.fori_loop(0, chunks, drain, 0)
+    if spill:
+        for j in range(1, ndev):
+            meta_copy(j).wait_send()
+
+
+def moe(hidden, rows, gates, meta, w_gate, w_up, w_down, ndev, main, spill):
+    toks, d_model = hidden.shape
+    experts, _, ff = w_gate.shape
+    crow = 2 * main
+    chunks = experts // 2 + (1 if spill else 0)
+    slots = 3 if spill else 2
+    vm = pl.BlockSpec(memory_space=pltpu.VMEM)
+    hbm = pl.BlockSpec(memory_space=pl.ANY)
+    bf16, f32 = jnp.bfloat16, jnp.float32
+    dma = pltpu.SemaphoreType.DMA
+    buf = pltpu.VMEM((chunks, ndev, crow, d_model), bf16)
+    tile_rows = 2 * ndev * main if spill else ndev * main
+    rows_lane = jnp.pad(rows.T, ((0, 6), (0, 0)), constant_values=-1)
+    return pl.pallas_call(
+        functools.partial(moe_block, main=main, spill=spill),
+        name='moe_spill' if spill else 'moe_full',
+        out_shape=jax.ShapeDtypeStruct((toks, d_model), bf16),
+        in_specs=[vm] * 5 + [hbm] * 3,
+        out_specs=vm,
+        scratch_shapes=[
+            buf, buf, buf, buf, pltpu.VMEM(meta.shape, f32),
+            pltpu.VMEM((tile_rows, d_model), bf16), pltpu.VMEM((tile_rows, d_model), f32), pltpu.VMEM((toks, d_model), f32),
+            pltpu.VMEM((slots, d_model, ff // 2), bf16), pltpu.VMEM((slots, d_model, ff // 2), bf16), pltpu.VMEM((slots, ff // 2, d_model), bf16),
+            dma((chunks, ndev)), dma((chunks, ndev)), dma((chunks, ndev)), dma((chunks, ndev)), dma((1,)), dma((ndev,)), dma((ndev,)), dma((slots, 3)),
+        ],
+        compiler_params=pltpu.CompilerParams(collective_id=1 if spill else 2, has_side_effects=True, vmem_limit_bytes=63 * MIB),
+        cost_estimate=pl.CostEstimate(flops=6 * tile_rows * experts * d_model * ff, bytes_accessed=6 * experts * d_model * ff, transcendentals=0),
+    )(hidden, rows_lane, rows, gates, meta, w_gate, w_up, w_down)
 
 
 def solution(mesh):
@@ -345,29 +600,36 @@
         exp_local = w_gate.shape[0]
         num_exp = exp_local * num_devs
         capacity = 4 * tok_dev // num_exp
+        mean = capacity // 2
+        crow = 2 * mean
         cp_rank = lax.axis_index('cp')
+        me = cp_rank * tp_size + lax.axis_index('tp')
+
+        flat = idx_blk.reshape(-1)
+        count = flat.shape[0]
+        onehot = flat[:, None] == jnp.arange(num_exp)[None, :]
+        before = (jnp.arange(count)[:, None] > jnp.arange(count)[None, :]).astype(jnp.bfloat16)
+        ranks = jnp.dot(before, onehot.astype(jnp.bfloat16), preferred_element_type=jnp.float32)
+        pos = jnp.sum(jnp.where(onehot, ranks, 0.0), axis=1).astype(jnp.int32)
+        dest, local = flat // exp_local, flat % exp_local
+        over = pos >= mean
+        onehot = (dest[:, None] == jnp.arange(num_devs)[None, :]) & over[:, None]
+        ranks = jnp.dot(before, onehot.astype(jnp.bfloat16), preferred_element_type=jnp.float32)
+        spill_pos = jnp.sum(jnp.where(onehot, ranks, 0.0), axis=1).astype(jnp.int32)
+        flag = jnp.full((8, 128), jnp.max(jnp.sum(onehot.astype(jnp.float32), axis=0)))
+        rows_spill = jnp.where(over, dest * crow + spill_pos, ((1 + local // 2) * num_devs + dest) * crow + (local % 2) * mean + pos)
+        rows_full = ((local // 2) * num_devs + dest) * (2 * capacity) + (local % 2) * capacity + pos
+        slot = jnp.arange(num_devs * crow)
+        code = jnp.sum(jnp.where((rows_spill[:, None] == slot[None, :]) & over[:, None], (1 + local * mean + pos - mean)[:, None], 0), axis=0).astype(jnp.float32)
+        meta = jnp.where(slot[None, :] // crow == me, jnp.tile(code.reshape(num_devs, crow), (1, num_devs)), 0.0)
+        meta = jnp.broadcast_to(meta[:, None, :], (num_devs, 8, num_devs * crow))
 
         w_qkv = jnp.concatenate([lax.dynamic_slice_in_dim(w, cp_rank * heads, heads, 1).reshape(d_model, width) for w in (w_q, w_k, w_v)], axis=1)
-        hidden = attention_block(x_blk, w_qkv, w_o.reshape(-1, d_model), heads, head_dim, num_devs)
-
-        flat_ids = idx_blk.reshape(-1)
-        num_flat = flat_ids.shape[0]
-        onehot = (flat_ids[:, None] == jnp.arange(num_exp)[None, :])
-        before = (jnp.arange(num_flat)[:, None] > jnp.arange(num_flat)[None, :]).astype(jnp.bfloat16)
-        ranks = jnp.dot(before, onehot.astype(jnp.bfloat16), preferred_element_type=jnp.float32)
-        slot_pos = jnp.sum(jnp.where(onehot, ranks, 0.0), axis=1).astype(jnp.int32)
-        slot_ids = (flat_ids * capacity + slot_pos).reshape(tok_dev, 2)
-        select = (slot_ids[:, :, None] == jnp.arange(num_exp * capacity)[None, None, :]).astype(jnp.bfloat16)
-        send_buf = jnp.einsum('tkn,tm->nm', select, hidden, preferred_element_type=jnp.float32).astype(jnp.bfloat16)
-        recv_buf = lax.all_to_all(send_buf, ('cp', 'tp'), 0, 0, tiled=True)
-        tok_in = recv_buf.reshape(num_devs, exp_local, capacity, -1)
-        gate_pre = jnp.einsum('secm,emf->secf', tok_in, w_gate, preferred_element_type=jnp.float32)
-        up_pre = jnp.einsum('secm,emf->secf', tok_in, w_up, preferred_element_type=jnp.float32)
-        hid_act = (jax.nn.silu(gate_pre) * up_pre).astype(jnp.bfloat16)
-        exp_out = jnp.einsum('secf,efm->secm', hid_act, w_down, preferred_element_type=jnp.float32).astype(jnp.bfloat16)
-        back_buf = lax.all_to_all(exp_out.reshape(num_devs * exp_local * capacity, -1), ('cp', 'tp'), 0, 0, tiled=True)
-        picked = jnp.einsum('tkn,nm->tkm', select, back_buf, preferred_element_type=jnp.float32)
-        moe_out = jnp.sum(gate_blk[:, :, None] * picked, axis=1)
-        return (hidden.astype(jnp.float32) + moe_out).astype(jnp.bfloat16)
+        hidden, most = attention_block(x_blk, w_qkv, w_o.reshape(-1, d_model), flag, heads, head_dim, num_devs)
+
+        def run(rows, main, spill):
+            return lambda h: moe(h, rows.reshape(tok_dev, 2), gate_blk, meta, w_gate, w_up, w_down, num_devs, main, spill)
+
+        return lax.cond(most[0, 0] <= crow, run(rows_spill, mean, True), run(rows_full, capacity, False), hidden)
 
     return jax.shard_map(device_fn, mesh=mesh, in_specs=(row_spec, head_spec, head_spec, head_spec, wo_spec, row_spec, row_spec, expert_spec, expert_spec, expert_spec), out_specs=row_spec, check_vma=False)

time: 450 us -> 302 us (0.67)
  blocking collectives: 198 us -> 0 us
  Pallas kernels: 144 us -> 274 us
  matrix products: 78.4 us -> 1.07 us
    all_to_all x2 -> x0, blocking collectives: 198 us -> none  [the longest x1 102 us: device_fn(): recv_buf = lax.all_to_all(send_buf, ('cp', 'tp'), 0, 0, tiled=True)]
    pallas_call x0 -> x1, Pallas kernels: none -> 131 us  [moe(): pl.pallas_call(functools.partial(moe_block, main=main, spill=spill), name...]
    dot_general x5 -> x0, matrix products: 77.8 us -> none  [the longest x1 22.8 us: device_fn(): jnp.einsum('secm,emf->secf', tok_in, w_up, preferred_element_type=jnp.flo...]
    convert_element_type x3 -> x1, local copies, waits for them, and re-layouts: 8.56 us -> 0.08 us  [device_fn(): jnp.sum(jnp.where((rows_spill[:, None] == slot[None, :]) & over[:, None],...]
where the time goes in v3:
time: 302 us; the launch traced here: 300 us
  Pallas kernels  274 us (91%)
  local copies, waits for them, and re-layouts  19.5 us (6%)
  other arithmetic  4.43 us (1%)
    pallas_call x1, Pallas kernels, attention_block(): pl.pallas_call(functools.partial(attn_block, heads=heads, head_dim=head_d...  144 us
    pallas_call x1, Pallas kernels, moe(): pl.pallas_call(functools.partial(moe_block, main=main, spill=spill), name...  131 us
    dynamic_slice x2, local copies, waits for them, and re-layouts, device_fn(): lax.dynamic_slice_in_dim(w, cp_rank * heads, heads, 1)  6.17 us

profile of v3, /device:TPU:0, one launch (start us, length us, event | category | flops | bytes accessed | tf_op | source)
XLA Modules:
  0.0 300.5 jit_solution(8431676501377728693)
XLA Ops:
  0.0 3.7 %constant_dynamic-slice_fusion = (bf16[2048,2,128]{2,1,0:T(2,128)(2,1)S(1)}, bf16[2048,2,128]{2,1,0:T(2,128)(2,1)S(1)}) fusion(bf16[2048,4,128]{2,1,0:T(4,128)(2,1)} %param.15, s32[]{:T(128)S(6)} %select_n.90, bf16[2048,4,128]{2,1,0:T(4,128)(2,1)} %param.14), kind=kLoop, calls=%fused_computation.45 | loop fusion | bytes 4194308 | tf_op jit(solution)/shard_map/dynamic_slice | solution.py:627
  3.7 0.8 copy.40
  4.6 1.3 copy.34
  5.9 0.8 copy.41
  6.7 1.3 copy.35
  8.0 0.0 copy-start
  8.0 2.4 constant_dynamic-slice_fusion.2
  10.4 0.8 copy.39
  11.2 0.5 copy.33
  11.8 0.0 copy-done
  11.8 0.0 copy-start.4
  11.8 2.8 pad_maximum_fusion.wqkv_ref
  14.6 0.0 copy-done.4
  14.6 0.1 copy.36
  14.8 0.2 reshape.211
  14.9 0.6 fusion.3
  15.6 0.1 convert_reduce_fusion
  15.7 0.6 reduce_max.9
  16.3 1.1 broadcast_in_dim.53.flag_ref
  17.4 0.0 copy-start.3
  17.4 143.6 %attn_block.1 = (bf16[512,2048]{1,0:T(8,128)(2,1)}, f32[8,128]{1,0:T(8,128)}) custom-call(bf16[512,2048]{1,0:T(8,128)(2,1)} %x_hbm.1, bf16[2048,768]{1,0:T(8,128)(2,1)} %pad_maximum_fusion.wqkv_ref, bf16[512,2048]{1,0:T(8,128)(2,1)} %bitcast.12, f32[8,128]{1,0:T(8,128)} %broadcast_in_dim.53.flag_ref), custom_call_target="tpu_custom_call" | custom-call | flops 30064771072 | bytes 16777216 | tf_op jit(solution)/shard_map/attn_block/pallas_call | solution.py:328
  161.0 0.5 fusion.5
  161.5 0.8 select_reduce_fusion
  162.4 0.1 convert_element_type.48
  162.5 0.1 tile.9
  162.6 1.2 slice.3
  164.5 0.0 copy-done.3
  164.5 132.8 %conditional.1 = (bf16[512,2048]{1,0:T(8,128)(2,1)}) conditional(s32[]{:T(128)} %bitcast.6, (s32[1024]{0:T(1024)S(1)}, s32[1024]{0:T(1024)S(1)}, s32[1024]{0:T(1024)S(1)}, s32[1024]{0:T(1024)S(1)}, s32[1024]{0:T(1024)S(1)}, /*index=5*/s32[1024]{0:T(1024)S(1)}, bf16[512,2048]{1,0:T(8,128)(2,1)}, f32[512,2]{0,1:T(2,128)S(1)}, ...), branch_computations={%region_5.6_spmd, %region_6.7_spmd} | conditional | flops 25769816064 | bytes 100761640 | solution.py:633
  164.7 0.2 reshape.201.rc_ref
  164.9 0.0 copy-start.2
  164.9 0.1 copy.29
  165.0 0.6 pad.6.rl_ref
  165.6 0.9 copy.38.g_ref
  166.5 0.0 copy-done.2
  166.5 130.8 %moe_spill.2 = bf16[512,2048]{1,0:T(8,128)(2,1)} custom-call(bf16[512,2048]{1,0:T(8,128)(2,1)} %get-tuple-element.143.h_ref, s32[8,512]{1,0:T(8,128)} %pad.6.rl_ref, s32[512,2]{1,0:T(8,128)} %copy-done.2, f32[512,2]{1,0:T(8,128)} %copy.38.g_ref, f32[8,8,256]{2,1,0:T(8,128)S(1)} %get-tuple-element.153.meta_ref, ...), custom_call_target="tpu_custom_call" | custom-call | flops 25769803776 | bytes 100663296 | tf_op jit(solution)/shard_map/cond/branch_1_fun/moe_spill/pallas_call | solution.py:569
  297.3 3.2 %copy.45 = bf16[512,2048]{1,0:T(8,128)(2,1)} copy(bf16[512,2048]{1,0:T(8,128)(2,1)} %get-tuple-element.161) | data formatting | bytes 4194304
  (14 shorter events, 0.1 us)
Async XLA Ops:
  8.0 3.8 %copy-start = (bf16[2048,256]{1,0:T(8,128)(2,1)S(1)}, bf16[2048,256]{1,0:T(8,128)(2,1)}, u32[]{:S(2)}) copy-start(bf16[2048,256]{1,0:T(8,128)(2,1)} %copy.34) | copy-start | bytes 3145732
  11.8 2.8 copy-start.4
  17.4 147.1 %copy-start.3 = (f32[512,2]{0,1:T(2,128)S(1)}, f32[512,2]{0,1:T(2,128)}, u32[]{:S(2)}) copy-start(f32[512,2]{0,1:T(2,128)} %param.18) | copy-start | bytes 12292
  164.9 1.6 copy-start.2

commit v4 on v3

--- a/solution.py
+++ b/solution.py
@@ -20,7 +20,7 @@
     return out
 
 
-def attn_block(x_hbm, wqkv_ref, wo_hbm, flag_ref, h_ref, any_ref, xbuf, qkv, s_ref, acc_ref, o_loc, o_cat, wo_buf,
+def attn_block(x_hbm, wq_hbm, wk_hbm, wv_hbm, wo_hbm, flag_ref, h_ref, any_ref, xbuf, wqkv_ref, w_pair, qkv, s_ref, acc_ref, o_loc, o_cat, wo_buf,
                flags, loc_sem, xs, xr, ws, wr, os_sem, or_sem, fs, fr, *, heads, head_dim):
     cp, tp = lax.axis_index('cp'), lax.axis_index('tp')
     xx, cc = tp // 2, tp % 2
@@ -42,13 +42,12 @@
     def dev(dx, dy, dc):
         return {'cp': (cp + dy) % 2, 'tp': tp_of(dx, dc)}
 
-    XN, YN, CN, DG = (1, 0, 0), (0, 1, 0), (0, 0, 1), (1, 1, 0)
-    XC, YC, DC = (1, 0, 1), (0, 1, 1), (1, 1, 1)
-
     x_load = pltpu.make_async_copy(x_hbm, xbuf.at[me], loc_sem.at[0])
     wo_load = pltpu.make_async_copy(wo_hbm, wo_buf.at[pl.ds(tp * wrows, wrows)], loc_sem.at[1])
     x_load.start()
     wo_load.start()
+    w_loads = [pltpu.make_async_copy(w.at[:, pl.ds(heads * cp, heads), :], w_pair, loc_sem.at[2]) for w in (wq_hbm, wk_hbm, wv_hbm)]
+    w_loads[0].start()
 
     barrier = pltpu.get_barrier_semaphore()
     for k in range(1, ndev):
@@ -57,15 +56,22 @@
     pl.semaphore_wait(barrier, ndev - 1)
 
     def xcopy(slot, owner, row0, count, part, target):
-        ref = xbuf.at[idx(*owner), pl.ds(row0, count)]
+        ref = xbuf.at[idx(*owner), pl.ds(row0 if isinstance(row0, int) else pl.multiple_of(row0, quarter), count)]
         return pltpu.make_async_remote_copy(src_ref=ref, dst_ref=ref, send_sem=xs.at[slot], recv_sem=xr.at[idx(*owner), part], device_id=dev(*target), device_id_type=MESH)
 
-    sent = []
-
-    def send(*args):
-        copy = xcopy(*args)
-        copy.start()
-        sent.append(copy)
+    XN, YN, CN, DG, OWN = (1, 0, 0), (0, 1, 0), (0, 0, 1), (1, 1, 0), (0, 0, 0)
+    XC, YC, DC = (1, 0, 1), (0, 1, 1), (1, 1, 1)
+    H, Q = half_rows, quarter
+    sends = [
+        (OWN, 0, H, 0, XN), (OWN, H, Q, 2, XN), (OWN, 0, H, 0, YN), (OWN, H, Q, 2, YN), (OWN, 0, H, 0, CN), (OWN, H, H, 2, CN),
+        (XN, 0, H, 0, CN), (XN, H, H, 2, CN), (YN, 0, H, 0, CN), (YN, H, H, 2, CN),
+        (YN, 0, Q, 0, XN), (YN, H, Q, 2, XN), (XN, Q, Q, 1, YN), (XN, H + Q, Q, 3, YN),
+        (DG, 0, H, 0, CN), (DG, H, H, 2, CN), (OWN, H + Q, Q, 3, XN), (OWN, H + Q, Q, 3, YN),
+    ]
+
+    def send(*slots):
+        for slot in slots:
+            xcopy(slot, *sends[slot]).start()
 
     def arrive(owner, row0, count, part):
         xcopy(0, owner, row0, count, part, CN).wait_recv()
@@ -81,15 +87,25 @@
     for j in range(1, ndev):
         flag_copy(j).start()
 
-    own = (0, 0, 0)
     x_load.wait()
-    for half in range(2):
-        send(0 + half, own, half * half_rows, half_rows, 2 * half, XN)
-        send(2 + half, own, half * half_rows, half_rows, 2 * half, YN)
-        send(4 + half, own, half * half_rows, half_rows, 2 * half, CN)
+    send(0, 2, 4, 1, 3, 5)
     wo_load.wait()
     w_own = wcopy(0, tp, 0, wrows, 0, CN)
     w_own.start()
+
+    for kind in range(3):
+        w_loads[kind].wait()
+
+        def relayout(n, _):
+            r = pl.ds(pl.multiple_of(n * 256, 256), 256)
+            for h in range(heads):
+                c = kind * width + h * head_dim
+                wqkv_ref[r, c:c + head_dim] = w_pair[r, h, :]
+            return 0
+
+        lax.fori_loop(0, d_model // 256, relayout, 0)
+        if kind < 2:
+            w_loads[kind + 1].start()
 
     def project(owner, half):
         r, t = owner // 4, owner % 4
@@ -112,48 +128,64 @@
 
     lax.fori_loop(0, 4, near, 0)
 
-    for half in range(2):
-        base = half * half_rows
-        arrive(XN, base, half_rows, 2 * half)
-        send(6 + half, XN, base, half_rows, 2 * half, CN)
-        send(12 + half, XN, base + quarter, quarter, 2 * half + 1, YN)
-        arrive(YN, base, half_rows, 2 * half)
-        send(8 + half, YN, base, half_rows, 2 * half, CN)
-        send(10 + half, YN, base, quarter, 2 * half, XN)
+    w_x = [(1 + k, tp, cp * whalf + k * wquart, wquart, 1 + k, XN) for k in range(2)]
+
+    def gather(p):
+        base = p * half_rows
+
+        @pl.when(p == 0)
+        def _():
+            arrive(XN, 0, H, 0)
+            arrive(YN, 0, H, 0)
+            send(12, 10, 16, 17, 6, 8)
 
         def mid(u, _):
             @pl.when(u == 2)
             def _():
-                arrive(XC, base, half_rows, 2 * half)
+                arrive(XC, base, H, 2 * p)
 
             @pl.when(u == 3)
             def _():
-                arrive(YC, base, half_rows, 2 * half)
-
-            project(idx(1 - u % 2, u % 2, u // 2), half)
+                arrive(YC, base, H, 2 * p)
+
+            project(idx(1 - u % 2, u % 2, u // 2), p)
             return 0
 
         lax.fori_loop(0, 4, mid, 0)
 
-    w_x = [wcopy(1 + k, tp, cp * whalf + k * wquart, wquart, 1 + k, XN) for k in range(2)]
-    for copy in w_x:
-        copy.start()
-
-    for half in range(2):
-        base = half * half_rows
-        arrive(DG, base, quarter, 2 * half)
-        arrive(DG, base + quarter, quarter, 2 * half + 1)
-        send(14 + half, DG, base, half_rows, 2 * half, CN)
+        @pl.when(p == 0)
+        def _():
+            arrive(XN, H, Q, 2)
+            arrive(YN, H, Q, 2)
+            send(11)
+
+        arrive(DG, base, Q, 2 * p)
+        arrive(DG, base + Q, Q, 2 * p + 1)
+
+        @pl.when(p == 0)
+        def _():
+            send(14)
+
+        @pl.when(p == 1)
+        def _():
+            send(15)
 
         def far(u, _):
             @pl.when(u == 1)
             def _():
-                arrive(DC, base, half_rows, 2 * half)
-
-            project(idx(1, 1, u), half)
+                arrive(DC, base, H, 2 * p)
+
+            project(idx(1, 1, u), p)
             return 0
 
         lax.fori_loop(0, 2, far, 0)
+
+    def late():
+        arrive(XN, H + Q, Q, 3)
+        arrive(YN, H + Q, Q, 3)
+        send(13, 7, 9)
+        for spec in w_x:
+            wcopy(*spec).start()
 
     coef = (head_dim ** -0.5) * math.log2(math.e)
     my_col = (4 * tp + 2 * cp) * head_dim
@@ -205,17 +237,19 @@
     blocks = seq // QB
 
     def q_step(i, _):
-        @pl.when(i == blocks - 3)
+        @pl.when(i == blocks // 2 - 1)
+        def _():
+            late()
+            for early in range(blocks // 2 - 1):
+                o_send(early)
+
+        @pl.when(i == blocks - 2)
         def _():
             w_pass(0)
 
-        @pl.when(i == blocks - 2)
+        @pl.when(i == blocks - 1)
         def _():
             w_pass(1)
-
-        @pl.when(i == blocks - 1)
-        def _():
-            w_last(0)
 
         q_rows = pl.ds(pl.multiple_of(i * QB, QB), QB)
 
@@ -256,11 +290,21 @@
         for h in range(heads):
             total = jnp.sum(ls[h], axis=1, keepdims=True)
             o_loc[q_rows, h * head_dim:(h + 1) * head_dim] = (acc_ref[h] / total).astype(jnp.bfloat16)
-        o_send(i)
-        return 0
-
-    lax.fori_loop(0, blocks, q_step, 0)
-
+
+        @pl.when(i >= blocks // 2 - 1)
+        def _():
+            o_send(i)
+
+        return 0
+
+    def phase(p, _):
+        gather(p)
+        lax.fori_loop(p * (blocks // 2), (p + 1) * (blocks // 2), q_step, 0)
+        return 0
+
+    lax.fori_loop(0, 2, phase, 0)
+
+    w_last(0)
     w_last(1)
     wcopy(1, tp_of(0, 1), 0, wrows, 0, CN).wait_recv()
     for k in range(2):
@@ -306,18 +350,18 @@
         flag_copy(j).wait_send()
     any_ref[...] = most
 
-    for copy in sent:
-        copy.wait_send()
+    for slot in range(len(sends)):
+        xcopy(slot, *sends[slot]).wait_send()
     w_own.wait_send()
-    for copy in w_x:
-        copy.wait_send()
+    for spec in w_x:
+        wcopy(*spec).wait_send()
     for k in range(2):
         wcopy(3 + k, peer_t, cp * whalf + k * wquart, wquart, 3 + k, YN).wait_send()
         wcopy(5 + k, peer_t, cp * whalf + k * wquart, wquart, 5 + k, CN).wait_send()
         wcopy(7 + k, peer_t, (1 - cp) * whalf + k * wquart, wquart, 7 + k, CN).wait_send()
 
 
-def attention_block(x_blk, w_qkv, w_o, flag, heads, head_dim, ndev):
+def attention_block(x_blk, w_q, w_k, w_v, w_o, flag, heads, head_dim, ndev):
     rows, d_model = x_blk.shape
     seq = rows * ndev
     width = heads * head_dim
@@ -329,19 +373,19 @@
         functools.partial(attn_block, heads=heads, head_dim=head_dim),
         name='attn_block',
         out_shape=(jax.ShapeDtypeStruct((rows, d_model), bf16), jax.ShapeDtypeStruct(flag.shape, f32)),
-        in_specs=[hbm, vm, hbm, vm],
+        in_specs=[hbm] * 5 + [vm],
         out_specs=(vm, vm),
         scratch_shapes=[
-            pltpu.VMEM((ndev, rows, d_model), bf16), pltpu.VMEM((seq, 3 * width), bf16),
+            pltpu.VMEM((ndev, rows, d_model), bf16), pltpu.VMEM((d_model, 3 * width), bf16), pltpu.VMEM((d_model, heads, head_dim), bf16), pltpu.VMEM((seq, 3 * width), bf16),
             pltpu.VMEM((heads, QB, seq), f32), pltpu.VMEM((heads, QB, head_dim), f32),
             pltpu.VMEM((seq, width), bf16), pltpu.VMEM((rows, ndev * width), bf16),
             pltpu.VMEM((ndev * width, d_model), bf16),
             pltpu.VMEM((ndev,) + flag.shape, f32),
-            dma((2,)), dma((16,)), dma((ndev, 4)), dma((9,)), dma((9,)), dma((16,)), dma((ndev, 2)), dma((ndev,)), dma((ndev,)),
+            dma((3,)), dma((18,)), dma((ndev, 4)), dma((9,)), dma((9,)), dma((16,)), dma((ndev, 2)), dma((ndev,)), dma((ndev,)),
         ],
         compiler_params=pltpu.CompilerParams(collective_id=0, has_side_effects=True, vmem_limit_bytes=63 * MIB),
         cost_estimate=pl.CostEstimate(flops=2 * seq * d_model * width * 3 + 4 * seq * seq * width, bytes_accessed=16 * MIB, transcendentals=0),
-    )(x_blk, w_qkv, w_o, flag)
+    )(x_blk, w_q, w_k, w_v, w_o, flag)
 
 
 def moe_block(h_ref, rl_ref, rc_ref, g_ref, meta_ref, wg_hbm, wu_hbm, wd_hbm, y_ref, send, recv, zbuf, ret,
@@ -596,7 +640,6 @@
         tok_dev, d_model = x_blk.shape
         heads_tp, head_dim = w_q.shape[1], w_q.shape[2]
         heads = heads_tp // cp_size
-        width = heads * head_dim
         exp_local = w_gate.shape[0]
         num_exp = exp_local * num_devs
         capacity = 4 * tok_dev // num_exp
@@ -624,8 +667,7 @@
         meta = jnp.where(slot[None, :] // crow == me, jnp.tile(code.reshape(num_devs, crow), (1, num_devs)), 0.0)
         meta = jnp.broadcast_to(meta[:, None, :], (num_devs, 8, num_devs * crow))
 
-        w_qkv = jnp.concatenate([lax.dynamic_slice_in_dim(w, cp_rank * heads, heads, 1).reshape(d_model, width) for w in (w_q, w_k, w_v)], axis=1)
-        hidden, most = attention_block(x_blk, w_qkv, w_o.reshape(-1, d_model), flag, heads, head_dim, num_devs)
+        hidden, most = attention_block(x_blk, w_q, w_k, w_v, w_o.reshape(-1, d_model), flag, heads, head_dim, num_devs)
 
         def run(rows, main, spill):
             return lambda h: moe(h, rows.reshape(tok_dev, 2), gate_blk, meta, w_gate, w_up, w_down, num_devs, main, spill)

time: 302 us -> 281 us (0.930)
  local copies, waits for them, and re-layouts: 19.5 us -> 8.59 us
  Pallas kernels: 274 us -> 267 us
    pallas_call x1, Pallas kernels: 131 us -> 123 us  [moe(): pl.pallas_call(functools.partial(moe_block, main=main, spill=spill), name...]
    dynamic_slice x2 -> x0, local copies, waits for them, and re-layouts: 6.17 us -> none  [device_fn(): lax.dynamic_slice_in_dim(w, cp_rank * heads, heads, 1)]
    reshape x3 -> x0, local copies, waits for them, and re-layouts: 3.16 us -> none  [device_fn(): lax.dynamic_slice_in_dim(w, cp_rank * heads, heads, 1)]
where the time goes in v4:
time: 281 us; the launch traced here: 279 us
  Pallas kernels  267 us (95%)
  local copies, waits for them, and re-layouts  8.59 us (3%)
    pallas_call x1, Pallas kernels, attention_block(): pl.pallas_call(functools.partial(attn_block, heads=heads, head_dim=head_d...  144 us
    pallas_call x1, Pallas kernels, moe(): pl.pallas_call(functools.partial(moe_block, main=main, spill=spill), name...  123 us

profile of v4, /device:TPU:0, one launch (start us, length us, event | category | flops | bytes accessed | tf_op | source)
XLA Modules:
  0.0 279.2 jit_solution(18371402803963927942)
XLA Ops:
  0.0 0.8 copy.24
  0.8 0.2 reshape.199
  1.0 0.6 fusion.3
  1.6 0.1 convert_reduce_fusion
  1.8 0.7 reduce_max.9
  2.5 1.3 broadcast_in_dim.53.flag_ref
  3.7 0.5 fusion.5
  4.3 0.8 select_reduce_fusion
  5.1 0.1 convert_element_type.48
  5.2 0.1 tile.9
  5.3 0.0 copy-start.2
  5.3 143.6 %attn_block.1 = (bf16[512,2048]{1,0:T(8,128)(2,1)}, f32[8,128]{1,0:T(8,128)}) custom-call(bf16[512,2048]{1,0:T(8,128)(2,1)} %x_hbm.1, bf16[2048,4,128]{2,1,0:T(4,128)(2,1)} %wq_hbm.1, bf16[2048,4,128]{2,1,0:T(4,128)(2,1)} %wk_hbm.1, bf16[2048,4,128]{2,1,0:T(4,128)(2,1)} %wv_hbm.1, bf16[512,2048]{1,0:T(8,128)(2,1)} %bitcast.6, f32[8,128]{1,0:T(8,128)} %broadcast_in_dim.53.flag_ref), custom_call_target="tpu_custom_call" | custom-call | flops 30064771072 | bytes 16777216 | tf_op jit(solution)/shard_map/attn_block/pallas_call | solution.py:372
  148.9 1.2 slice.3
  150.7 0.0 copy-done.2
  150.8 125.3 %conditional.1 = (bf16[512,2048]{1,0:T(8,128)(2,1)}) conditional(s32[]{:T(128)} %bitcast.3, (s32[1024]{0:T(1024)S(1)}, s32[1024]{0:T(1024)S(1)}, s32[1024]{0:T(1024)S(1)}, s32[1024]{0:T(1024)S(1)}, s32[1024]{0:T(1024)S(1)}, /*index=5*/s32[1024]{0:T(1024)S(1)}, bf16[512,2048]{1,0:T(8,128)(2,1)}, f32[512,2]{0,1:T(2,128)S(1)}, ...), branch_computations={%region_5.6_spmd, %region_6.7_spmd} | conditional | flops 25769816064 | bytes 100761640 | solution.py:675
  151.0 0.2 reshape.195.rc_ref
  151.2 0.0 copy-start.1
  151.2 0.1 copy.23
  151.3 0.6 pad.6.rl_ref
  151.9 0.8 copy.26.g_ref
  152.8 0.0 copy-done.1
  152.8 123.3 %moe_spill.2 = bf16[512,2048]{1,0:T(8,128)(2,1)} custom-call(bf16[512,2048]{1,0:T(8,128)(2,1)} %get-tuple-element.143.h_ref, s32[8,512]{1,0:T(8,128)} %pad.6.rl_ref, s32[512,2]{1,0:T(8,128)} %copy-done.1, f32[512,2]{1,0:T(8,128)} %copy.26.g_ref, f32[8,8,256]{2,1,0:T(8,128)S(1)} %get-tuple-element.153.meta_ref, ...), custom_call_target="tpu_custom_call" | custom-call | flops 25769803776 | bytes 100663296 | tf_op jit(solution)/shard_map/cond/branch_1_fun/moe_spill/pallas_call | solution.py:613
  276.1 3.2 %copy.30 = bf16[512,2048]{1,0:T(8,128)(2,1)} copy(bf16[512,2048]{1,0:T(8,128)(2,1)} %get-tuple-element.161) | data formatting | bytes 4194304
  (14 shorter events, 0.1 us)
Async XLA Ops:
  5.3 145.5 %copy-start.2 = (f32[512,2]{0,1:T(2,128)S(1)}, f32[512,2]{0,1:T(2,128)}, u32[]{:S(2)}) copy-start(f32[512,2]{0,1:T(2,128)} %param.18) | copy-start | bytes 12292
  151.2 1.6 copy-start.1

commit v5 on v4

--- a/solution.py
+++ b/solution.py
@@ -243,7 +243,7 @@
             for early in range(blocks // 2 - 1):
                 o_send(early)
 
-        @pl.when(i == blocks - 2)
+        @pl.when(i == blocks - 3)
         def _():
             w_pass(0)
 
@@ -389,15 +389,17 @@
 
 
 def moe_block(h_ref, rl_ref, rc_ref, g_ref, meta_ref, wg_hbm, wu_hbm, wd_hbm, y_ref, send, recv, zbuf, ret,
-              meta_in, xs, zacc, acc, wg, wu, wd, ds, dr, rs, rr, ls, ms, mr, wsem, *, main, spill):
+              meta_in, sp_send, sp_recv, sp_z, sp_ret, pool_in, xs, zacc, acc, wg, wu, wd, ds, dr, rs, rr, ms, mr, sp_sem, sp_dr, pool_s, pool_r, sp_rs, sp_rr, wsem, *, main, spill):
     cp, tp = lax.axis_index('cp'), lax.axis_index('tp')
+    xx, cc = tp // 2, tp % 2
     me = cp * 4 + tp
     chunks, ndev, crow, d_model = send.shape
     rows_all = ndev * crow
     toks = h_ref.shape[0]
     experts = wg_hbm.shape[0]
     slots, _, ff_half = wg.shape
-    first = 1 if spill else 0
+    sp_rows = sp_send.shape[1]
+    sp_base = chunks * rows_all
     steps = 2 * experts
     tile = 512
     f32, bf16 = jnp.float32, jnp.bfloat16
@@ -427,8 +429,40 @@
         pl.semaphore_signal(barrier, inc=1, device_id=dev(peer_of(j)), device_id_type=MESH)
     pl.semaphore_wait(barrier, ndev - 1)
 
+    AWAY = [(1, 0), (0, 1), (1, 1)]
+
+    def chip(dx, dy):
+        return ((cp + dy) % 2) * 2 + (xx + dx) % 2
+
+    def idx(dx, dy, dc):
+        return chip(dx, dy) * 2 + (cc + dc) % 2
+
+    def sp_copy(src, dst, ssem, rsem, target):
+        return pltpu.make_async_remote_copy(src_ref=src, dst_ref=dst, send_sem=ssem, recv_sem=rsem, device_id=dev(idx(*target)), device_id_type=MESH)
+
+    def sp_out(n):
+        if n < 3:
+            return sp_copy(sp_send.at[chip(*AWAY[n])], sp_recv.at[me], sp_sem.at[n], sp_dr.at[me], AWAY[n] + (0,))
+        return sp_copy(sp_send.at[chip(0, 0)], sp_recv.at[me], sp_sem.at[3], sp_dr.at[me], (0, 0, 1))
+
+    def sp_pass(n):
+        ref = sp_recv.at[idx(*AWAY[n], 0)]
+        return sp_copy(ref, ref, sp_sem.at[4 + n], sp_dr.at[idx(*AWAY[n], 0)], (0, 0, 1))
+
+    def sp_arrived(source):
+        ref = sp_recv.at[idx(*source)]
+        sp_copy(ref, ref, sp_sem.at[0], sp_dr.at[idx(*source)], (0, 0, 1)).wait_recv()
+
+    def sp_pool(n):
+        side = ([(0, 0)] + AWAY)[n]
+        return sp_copy(sp_z.at[idx(*side, 1)], pool_in.at[n], pool_s.at[n], pool_r.at[n], (0, 0, 1))
+
+    def sp_back(n):
+        side = AWAY[n]
+        return sp_copy(sp_z.at[idx(*side, 0)], sp_ret.at[chip(0, 0)], sp_rs.at[n], sp_rr.at[chip(0, 0)], side + (0,))
+
     def meta_copy(j):
-        return pltpu.make_async_remote_copy(src_ref=meta_ref.at[peer_of(j)], dst_ref=meta_in.at[me], send_sem=ms.at[j], recv_sem=mr.at[me], device_id=dev(peer_of(j)), device_id_type=MESH)
+        return pltpu.make_async_remote_copy(src_ref=meta_ref.at[peer_of(j) // 2], dst_ref=meta_in.at[me], send_sem=ms.at[j], recv_sem=mr.at[me], device_id=dev(peer_of(j)), device_id_type=MESH)
 
     if spill:
         for j in range(1, ndev):
@@ -460,6 +494,20 @@
     out_way = (send, recv, ds, dr)
     back_way = (zbuf, ret, rs, rr)
 
+    def sp_own():
+        return pltpu.make_async_copy(sp_send.at[chip(0, 0)], sp_recv.at[me], sp_sem.at[7])
+
+    if spill:
+        ids = lax.broadcasted_iota(jnp.int32, (4 * sp_rows, toks), 0) + sp_base
+        pick = ((ids == rl_ref[0:1, :]) | (ids == rl_ref[1:2, :])).astype(f32).astype(bf16)
+
+        def sp_cols(n, _):
+            c = pl.ds(pl.multiple_of(n * tile, tile), tile)
+            sp_send[:, :, c] = jnp.dot(pick, h_ref[:, c], preferred_element_type=f32).astype(bf16).reshape(4, sp_rows, tile)
+            return 0
+
+        lax.fori_loop(0, d_model // tile, sp_cols, 0)
+
     def pack(k, _):
         ids = lax.broadcasted_iota(jnp.int32, (rows_all, toks), 0) + k * rows_all
         pick = ((ids == rl_ref[0:1, :]) | (ids == rl_ref[1:2, :])).astype(f32).astype(bf16)
@@ -476,6 +524,13 @@
         def _():
             begin(*out_way, k - 1)
 
+        if spill:
+            @pl.when(k == 0)
+            def _():
+                for n in range(4):
+                    sp_out(n).start()
+                sp_own().start()
+
         return 0
 
     lax.fori_loop(0, chunks, pack, 0)
@@ -484,20 +539,26 @@
     if spill:
         for j in range(1, ndev):
             p = peer_of(j)
-            pltpu.make_async_remote_copy(src_ref=meta_ref.at[p], dst_ref=meta_in.at[p], send_sem=ms.at[j], recv_sem=mr.at[p], device_id=dev(p), device_id_type=MESH).wait_recv()
-        arrived(*out_way, 0)
-        total = meta_ref[me]
+            pltpu.make_async_remote_copy(src_ref=meta_in.at[p], dst_ref=meta_in.at[p], send_sem=ms.at[j], recv_sem=mr.at[p], device_id=dev(p), device_id_type=MESH).wait_recv()
+        for n in range(3):
+            sp_arrived(AWAY[n] + (0,))
+            sp_pass(n).start()
+        sp_own().wait()
+        sp_arrived((0, 0, 1))
+        for n in range(3):
+            sp_arrived(AWAY[n] + (1,))
+        total = meta_ref[me // 2]
         for j in range(1, ndev):
             total = total + meta_in[peer_of(j)]
-        code = total[0:1, :].astype(jnp.int32) - 1
+        code = total[0:1, :].astype(jnp.int32) - 1 - cc * (experts * main)
         lane = lax.broadcasted_iota(jnp.int32, code.shape, 1)
-        place = (lane // crow) * main + (code & (main - 1))
+        place = (lane // sp_rows) * main + (code & (main - 1))
         owner = code // main
-        zbuf[0] = jnp.zeros((ndev, crow, d_model), bf16)
+        sp_z[...] = jnp.zeros_like(sp_z)
     body = ndev * main
 
     def expert(e, _):
-        k = first + e // 2
+        k = e // 2
         part = pl.ds(pl.multiple_of((e % 2) * main, main), main)
 
         @pl.when(e % 2 == 0)
@@ -506,12 +567,12 @@
 
         xs[0:body, :] = recv[k, :, part, :].reshape(body, d_model)
         if spill:
-            slot_id = lax.broadcasted_iota(jnp.int32, (body, rows_all), 0)
+            slot_id = lax.broadcasted_iota(jnp.int32, (body, ndev * sp_rows), 0)
             pick = ((slot_id == place) & (owner == e)).astype(f32).astype(bf16)
 
             def gather(n, _):
                 c = pl.ds(pl.multiple_of(n * tile, tile), tile)
-                xs[body:2 * body, c] = jnp.dot(pick, recv[0, :, :, c].reshape(rows_all, tile), preferred_element_type=f32).astype(bf16)
+                xs[body:2 * body, c] = jnp.dot(pick, sp_recv[:, :, c].reshape(ndev * sp_rows, tile), preferred_element_type=f32).astype(bf16)
                 return 0
 
             lax.fori_loop(0, d_model // tile, gather, 0)
@@ -541,7 +602,7 @@
                     zbuf[k, :, part, c] = z[0:body].reshape(ndev, main, tile)
                     if spill:
                         spread = lax.dot_general(pick, z[body:], (((0,), (0,)), ((), ())), preferred_element_type=f32)
-                        zbuf[0, :, :, c] = zbuf[0, :, :, c] + spread.astype(bf16).reshape(ndev, crow, tile)
+                        sp_z[:, :, c] = sp_z[:, :, c] + spread.astype(bf16).reshape(ndev, sp_rows, tile)
                 return 0
 
             lax.fori_loop(0, d_model // tile, down, 0)
@@ -553,35 +614,55 @@
         return 0
 
     lax.fori_loop(0, experts, expert, 0)
+    if spill:
+        for n in range(4):
+            sp_pool(n).start()
     begin(*back_way, chunks - 1)
+    acc[...] = jnp.zeros_like(acc)
+
+    def sp_home():
+        return pltpu.make_async_copy(sp_z.at[me], sp_ret.at[chip(0, 0)], sp_rs.at[3])
+
     if spill:
-        begin(*back_way, 0)
-
-    acc[...] = jnp.zeros_like(acc)
-
-    def combine(kk, _):
-        k = (kk + first) % chunks
+        for n in range(4):
+            sp_pool(n).wait_recv()
+            at = idx(*([(0, 0)] + AWAY)[n], 0)
+            sp_z[at] = sp_z[at] + pool_in[n]
+        for n in range(3):
+            sp_back(n).start()
+        sp_home().start()
+
+    def chosen(ids, z):
+        z0 = jnp.dot((ids == rc_ref[:, 0:1]).astype(f32).astype(bf16), z, preferred_element_type=f32)
+        z1 = jnp.dot((ids == rc_ref[:, 1:2]).astype(f32).astype(bf16), z, preferred_element_type=f32)
+        return g_ref[:, 0:1] * z0 + g_ref[:, 1:2] * z1
+
+    def combine(k, _):
         arrived(*back_way, k)
         ids = lax.broadcasted_iota(jnp.int32, (toks, rows_all), 1) + k * rows_all
-        pick0 = (ids == rc_ref[:, 0:1]).astype(f32).astype(bf16)
-        pick1 = (ids == rc_ref[:, 1:2]).astype(f32).astype(bf16)
 
         def cols(n, _):
             c = pl.ds(pl.multiple_of(n * tile, tile), tile)
-            z = ret[k, :, :, c].reshape(rows_all, tile)
-            z0 = jnp.dot(pick0, z, preferred_element_type=f32)
-            z1 = jnp.dot(pick1, z, preferred_element_type=f32)
-            acc[:, c] += g_ref[:, 0:1] * z0 + g_ref[:, 1:2] * z1
+            acc[:, c] += chosen(ids, ret[k, :, :, c].reshape(rows_all, tile))
             return 0
 
         lax.fori_loop(0, d_model // tile, cols, 0)
         return 0
 
     lax.fori_loop(0, chunks, combine, 0)
+    if spill:
+        sp_home().wait()
+        for n in range(3):
+            ref = sp_ret.at[chip(*AWAY[n])]
+            sp_copy(ref, ref, sp_rs.at[n], sp_rr.at[chip(*AWAY[n])], (0, 0, 1)).wait_recv()
 
     def finish(n, _):
         c = pl.ds(pl.multiple_of(n * tile, tile), tile)
-        y_ref[:, c] = (h_ref[:, c].astype(f32) + acc[:, c]).astype(bf16)
+        moe_out = acc[:, c]
+        if spill:
+            ids = lax.broadcasted_iota(jnp.int32, (toks, 4 * sp_rows), 1) + sp_base
+            moe_out += chosen(ids, sp_ret[:, :, c].reshape(4 * sp_rows, tile))
+        y_ref[:, c] = (h_ref[:, c].astype(f32) + moe_out).astype(bf16)
         return 0
 
     lax.fori_loop(0, d_model // tile, finish, 0)
@@ -595,13 +676,20 @@
     if spill:
         for j in range(1, ndev):
             meta_copy(j).wait_send()
+        for n in range(4):
+            sp_out(n).wait_send()
+            sp_pool(n).wait_send()
+        for n in range(3):
+            sp_pass(n).wait_send()
+            sp_back(n).wait_send()
 
 
 def moe(hidden, rows, gates, meta, w_gate, w_up, w_down, ndev, main, spill):
     toks, d_model = hidden.shape
     experts, _, ff = w_gate.shape
     crow = 2 * main
-    chunks = experts // 2 + (1 if spill else 0)
+    chunks = experts // 2
+    sp_rows = 2 * main if spill else 16
     slots = 3 if spill else 2
     vm = pl.BlockSpec(memory_space=pltpu.VMEM)
     hbm = pl.BlockSpec(memory_space=pl.ANY)
@@ -617,10 +705,13 @@
         in_specs=[vm] * 5 + [hbm] * 3,
         out_specs=vm,
         scratch_shapes=[
-            buf, buf, buf, buf, pltpu.VMEM(meta.shape, f32),
+            buf, buf, buf, buf, pltpu.VMEM((ndev,) + meta.shape[1:], f32),
+            pltpu.VMEM((4, sp_rows, d_model), bf16), pltpu.VMEM((ndev, sp_rows, d_model), bf16), pltpu.VMEM((ndev, sp_rows, d_model), bf16),
+            pltpu.VMEM((4, sp_rows, d_model), bf16), pltpu.VMEM((4, sp_rows, d_model), bf16),
             pltpu.VMEM((tile_rows, d_model), bf16), pltpu.VMEM((tile_rows, d_model), f32), pltpu.VMEM((toks, d_model), f32),
             pltpu.VMEM((slots, d_model, ff // 2), bf16), pltpu.VMEM((slots, d_model, ff // 2), bf16), pltpu.VMEM((slots, ff // 2, d_model), bf16),
-            dma((chunks, ndev)), dma((chunks, ndev)), dma((chunks, ndev)), dma((chunks, ndev)), dma((1,)), dma((ndev,)), dma((ndev,)), dma((slots, 3)),
+            dma((chunks, ndev)), dma((chunks, ndev)), dma((chunks, ndev)), dma((chunks, ndev)), dma((ndev,)), dma((ndev,)),
+            dma((8,)), dma((ndev,)), dma((4,)), dma((4,)), dma((4,)), dma((4,)), dma((slots, 3)),
         ],
         compiler_params=pltpu.CompilerParams(collective_id=1 if spill else 2, has_side_effects=True, vmem_limit_bytes=63 * MIB),
         cost_estimate=pl.CostEstimate(flops=6 * tile_rows * experts * d_model * ff, bytes_accessed=6 * experts * d_model * ff, transcendentals=0),
@@ -656,16 +747,19 @@
         pos = jnp.sum(jnp.where(onehot, ranks, 0.0), axis=1).astype(jnp.int32)
         dest, local = flat // exp_local, flat % exp_local
         over = pos >= mean
-        onehot = (dest[:, None] == jnp.arange(num_devs)[None, :]) & over[:, None]
+        chips = num_devs // 2
+        onehot = (dest[:, None] // 2 == jnp.arange(chips)[None, :]) & over[:, None]
         ranks = jnp.dot(before, onehot.astype(jnp.bfloat16), preferred_element_type=jnp.float32)
         spill_pos = jnp.sum(jnp.where(onehot, ranks, 0.0), axis=1).astype(jnp.int32)
         flag = jnp.full((8, 128), jnp.max(jnp.sum(onehot.astype(jnp.float32), axis=0)))
-        rows_spill = jnp.where(over, dest * crow + spill_pos, ((1 + local // 2) * num_devs + dest) * crow + (local % 2) * mean + pos)
+        main_rows = exp_local // 2 * num_devs * crow
+        rows_spill = jnp.where(over, main_rows + dest // 2 * crow + spill_pos, ((local // 2) * num_devs + dest) * crow + (local % 2) * mean + pos)
         rows_full = ((local // 2) * num_devs + dest) * (2 * capacity) + (local % 2) * capacity + pos
-        slot = jnp.arange(num_devs * crow)
-        code = jnp.sum(jnp.where((rows_spill[:, None] == slot[None, :]) & over[:, None], (1 + local * mean + pos - mean)[:, None], 0), axis=0).astype(jnp.float32)
-        meta = jnp.where(slot[None, :] // crow == me, jnp.tile(code.reshape(num_devs, crow), (1, num_devs)), 0.0)
-        meta = jnp.broadcast_to(meta[:, None, :], (num_devs, 8, num_devs * crow))
+        slot = main_rows + jnp.arange(chips * crow)
+        lane = jnp.arange(num_devs * crow)
+        code = jnp.sum(jnp.where((rows_spill[:, None] == slot[None, :]) & over[:, None], (1 + (dest % 2 * exp_local + local) * mean + pos - mean)[:, None], 0), axis=0).astype(jnp.float32)
+        meta = jnp.where(lane[None, :] // crow == me, jnp.tile(code.reshape(chips, crow), (1, num_devs)), 0.0)
+        meta = jnp.broadcast_to(meta[:, None, :], (chips, 8, num_devs * crow))
 
         hidden, most = attention_block(x_blk, w_q, w_k, w_v, w_o.reshape(-1, d_model), flag, heads, head_dim, num_devs)
 

time: 281 us -> 266 us (0.947)
  Pallas kernels: 267 us -> 253 us
    pallas_call x1, Pallas kernels: 123 us -> 115 us  [moe(): pl.pallas_call(functools.partial(moe_block, main=main, spill=spill), name...]
    pallas_call x1, Pallas kernels: 144 us -> 138 us  [attention_block(): pl.pallas_call(functools.partial(attn_block, heads=heads, head_dim=head_d...]
where the time goes in v5:
time: 266 us; the launch traced here: 265 us
  Pallas kernels  253 us (95%)
  local copies, waits for them, and re-layouts  8.6 us (3%)
    pallas_call x1, Pallas kernels, attention_block(): pl.pallas_call(functools.partial(attn_block, heads=heads, head_dim=head_d...  138 us
    pallas_call x1, Pallas kernels, moe(): pl.pallas_call(functools.partial(moe_block, main=main, spill=spill), name...  115 us

profile of v5, /device:TPU:0, one launch (start us, length us, event | category | flops | bytes accessed | tf_op | source)
XLA Modules:
  0.0 265.4 jit_solution(2430763436944104064)
XLA Ops:
  0.0 0.8 copy.24
  0.8 0.2 reshape.257
  1.0 0.6 fusion.9
  1.7 0.1 convert_reduce_fusion
  1.8 0.7 reduce_max.9
  2.5 0.5 fusion.11
  3.0 1.3 broadcast_in_dim.53.flag_ref
  4.3 0.8 select_reduce_fusion
  5.1 0.1 convert_element_type.48
  5.2 0.1 tile.9
  5.3 0.0 copy-start.2
  5.3 137.9 %attn_block.1 = (bf16[512,2048]{1,0:T(8,128)(2,1)}, f32[8,128]{1,0:T(8,128)}) custom-call(bf16[512,2048]{1,0:T(8,128)(2,1)} %x_hbm.1, bf16[2048,4,128]{2,1,0:T(4,128)(2,1)} %wq_hbm.1, bf16[2048,4,128]{2,1,0:T(4,128)(2,1)} %wk_hbm.1, bf16[2048,4,128]{2,1,0:T(4,128)(2,1)} %wv_hbm.1, bf16[512,2048]{1,0:T(8,128)(2,1)} %bitcast.6, f32[8,128]{1,0:T(8,128)} %broadcast_in_dim.53.flag_ref), custom_call_target="tpu_custom_call" | custom-call | flops 30064771072 | bytes 16777216 | tf_op jit(solution)/shard_map/attn_block/pallas_call | solution.py:372
  143.2 1.2 slice.3
  145.1 0.0 copy-done.2
  145.1 117.1 %conditional.1 = (bf16[512,2048]{1,0:T(8,128)(2,1)}) conditional(s32[]{:T(128)} %bitcast.3, (s32[1024]{0:T(1024)S(1)}, s32[1024]{0:T(1024)S(1)}, s32[1024]{0:T(1024)S(1)}, s32[1024]{0:T(1024)S(1)}, bf16[512,2048]{1,0:T(8,128)(2,1)}, /*index=5*/f32[512,2]{0,1:T(2,128)S(1)}, f32[4,8,256]{2,1,0:T(8,128)S(1)}, bf16[8,2048,1024]{2,1,0:T(8,128)(2,1)}, ...), branch_computations={%region_5.6_spmd, %region_6.7_spmd} | conditional | flops 25769820160 | bytes 100779048 | solution.py:769
  145.4 0.2 reshape.253.rc_ref
  145.6 0.0 copy-start.1
  145.6 0.1 copy.23
  145.7 0.6 pad.6.rl_ref
  146.3 0.8 copy.26.g_ref
  147.2 0.0 copy-done.1
  147.2 115.1 %moe_spill.2 = bf16[512,2048]{1,0:T(8,128)(2,1)} custom-call(bf16[512,2048]{1,0:T(8,128)(2,1)} %get-tuple-element.161.h_ref, s32[8,512]{1,0:T(8,128)} %pad.6.rl_ref, s32[512,2]{1,0:T(8,128)} %copy-done.1, f32[512,2]{1,0:T(8,128)} %copy.26.g_ref, f32[4,8,256]{2,1,0:T(8,128)S(1)} %get-tuple-element.176.meta_ref, ...), custom_call_target="tpu_custom_call" | custom-call | flops 25769803776 | bytes 100663296 | tf_op jit(solution)/shard_map/cond/branch_1_fun/moe_spill/pallas_call | solution.py:701
  262.3 3.2 %copy.30 = bf16[512,2048]{1,0:T(8,128)(2,1)} copy(bf16[512,2048]{1,0:T(8,128)(2,1)} %get-tuple-element.184) | data formatting | bytes 4194304
  (19 shorter events, 0.1 us)
Async XLA Ops:
  5.3 139.8 %copy-start.2 = (f32[512,2]{0,1:T(2,128)S(1)}, f32[512,2]{0,1:T(2,128)}, u32[]{:S(2)}) copy-start(f32[512,2]{0,1:T(2,128)} %param.18) | copy-start | bytes 12292
  145.6 1.6 copy-start.1

commit v6 on v5

--- a/solution.py
+++ b/solution.py
@@ -20,8 +20,8 @@
     return out
 
 
-def attn_block(x_hbm, wq_hbm, wk_hbm, wv_hbm, wo_hbm, flag_ref, h_ref, any_ref, xbuf, wqkv_ref, w_pair, qkv, s_ref, acc_ref, o_loc, o_cat, wo_buf,
-               flags, loc_sem, xs, xr, ws, wr, os_sem, or_sem, fs, fr, *, heads, head_dim):
+def attn_block(x_hbm, wq_hbm, wk_hbm, wv_hbm, wo_hbm, ids_ref, gates_ref, h_ref, any_ref, lane_ref, col_ref, meta_ref, xbuf, wqkv_ref, w_pair, qkv, s_ref, acc_ref, o_loc, o_cat, wo_buf,
+               flag_ref, flags, tall, loc_sem, xs, xr, ws, wr, os_sem, or_sem, fs, fr, *, heads, head_dim, experts):
     cp, tp = lax.axis_index('cp'), lax.axis_index('tp')
     xx, cc = tp // 2, tp % 2
     me = cp * 4 + tp
@@ -84,9 +84,6 @@
         peer = (me + j) % ndev
         return pltpu.make_async_remote_copy(src_ref=flag_ref, dst_ref=flags.at[me], send_sem=fs.at[j], recv_sem=fr.at[me], device_id={'cp': peer // 4, 'tp': peer % 4}, device_id_type=MESH)
 
-    for j in range(1, ndev):
-        flag_copy(j).start()
-
     x_load.wait()
     send(0, 2, 4, 1, 3, 5)
     wo_load.wait()
@@ -107,6 +104,55 @@
         if kind < 2:
             w_loads[kind + 1].start()
 
+    def tables():
+        toks = ids_ref.shape[1]
+        f32, bf16 = jnp.float32, jnp.bfloat16
+        cap = 4 * toks // experts
+        mean = cap // 2
+        per_dev = experts // ndev
+        chips = ndev // 2
+        crow = 2 * mean
+        base = per_dev // 2 * ndev * crow
+        before = (lax.broadcasted_iota(jnp.int32, (toks, toks), 0) < lax.broadcasted_iota(jnp.int32, (toks, toks), 1)).astype(f32).astype(bf16)
+
+        def ranks(keys, keep, size):
+            out, seen = [], jnp.zeros((size, 1), f32)
+            for key, ok in zip(keys, keep):
+                hot = jnp.where((lax.broadcasted_iota(jnp.int32, (size, toks), 0) == key) & ok, 1.0, 0.0)
+                prior = jnp.dot(hot.astype(bf16), before, preferred_element_type=f32) + seen
+                out.append(jnp.sum(hot * prior, axis=0, keepdims=True).astype(jnp.int32))
+                seen = seen + jnp.sum(hot, axis=1, keepdims=True)
+            return out, seen
+
+        ids = [ids_ref[c:c + 1, :] for c in range(2)]
+        pos, _ = ranks(ids, [i >= 0 for i in ids], experts)
+        over = [p >= mean for p in pos]
+        dest = [i // per_dev for i in ids]
+        local = [i - d * per_dev for i, d in zip(ids, dest)]
+        spot, seen = ranks([d // 2 for d in dest], over, 8)
+        flag_ref[...] = jnp.broadcast_to(jnp.max(seen, axis=0, keepdims=True), flag_ref.shape)
+        rows, full, codes = [], [], []
+        for p, v, d, l, q in zip(pos, over, dest, local, spot):
+            pair = l // 2 * ndev + d
+            rows.append(jnp.where(v, base + d // 2 * crow + q, pair * crow + l % 2 * mean + p))
+            full.append(pair * 2 * cap + l % 2 * cap + p)
+            codes.append(jnp.where(v, 1 + (d % 2 * per_dev + l) * mean + p - mean, 0))
+        for n, row in enumerate(rows + full):
+            lane_ref[n:n + 1, :] = row
+        tall[...] = jnp.zeros_like(tall)
+        for n, row in enumerate(rows + full + [gates_ref[c:c + 1, :] for c in range(2)]):
+            tall[n:n + 1, :] = row.astype(f32)
+        col_ref[...] = tall[...].T
+        lane = lax.broadcasted_iota(jnp.int32, (toks, ndev * crow), 1)
+        for chip in range(chips):
+            total = jnp.zeros(meta_ref.shape[1:], f32)
+            for c in range(2):
+                place = col_ref[:, c:c + 1].astype(jnp.int32) - (base + chip * crow) + me * crow
+                hot = ((place == lane) & (lane // crow == me)).astype(f32).astype(bf16)
+                code = jnp.broadcast_to(codes[c].astype(f32), (8, toks)).astype(bf16)
+                total += jnp.dot(code, hot, preferred_element_type=f32)
+            meta_ref[chip] = total
+
     def project(owner, half):
         r, t = owner // 4, owner % 4
         seg = r + half * (3 - 2 * r)
@@ -127,6 +173,9 @@
         return 0
 
     lax.fori_loop(0, 4, near, 0)
+    tables()
+    for j in range(1, ndev):
+        flag_copy(j).start()
 
     w_x = [(1 + k, tp, cp * whalf + k * wquart, wquart, 1 + k, XN) for k in range(2)]
 
@@ -348,7 +397,7 @@
         pltpu.make_async_remote_copy(src_ref=flag_ref, dst_ref=flags.at[peer], send_sem=fs.at[j], recv_sem=fr.at[peer], device_id=dev(0, 0, 1), device_id_type=MESH).wait_recv()
         most = jnp.maximum(most, flags[peer])
         flag_copy(j).wait_send()
-    any_ref[...] = most
+    any_ref[0, 0] = jnp.max(most).astype(jnp.int32)
 
     for slot in range(len(sends)):
         xcopy(slot, *sends[slot]).wait_send()
@@ -361,7 +410,7 @@
         wcopy(7 + k, peer_t, (1 - cp) * whalf + k * wquart, wquart, 7 + k, CN).wait_send()
 
 
-def attention_block(x_blk, w_q, w_k, w_v, w_o, flag, heads, head_dim, ndev):
+def attention_block(x_blk, w_q, w_k, w_v, w_o, ids, gates, heads, head_dim, ndev, experts):
     rows, d_model = x_blk.shape
     seq = rows * ndev
     width = heads * head_dim
@@ -370,25 +419,25 @@
     bf16, f32 = jnp.bfloat16, jnp.float32
     dma = pltpu.SemaphoreType.DMA
     return pl.pallas_call(
-        functools.partial(attn_block, heads=heads, head_dim=head_dim),
+        functools.partial(attn_block, heads=heads, head_dim=head_dim, experts=experts),
         name='attn_block',
-        out_shape=(jax.ShapeDtypeStruct((rows, d_model), bf16), jax.ShapeDtypeStruct(flag.shape, f32)),
-        in_specs=[hbm] * 5 + [vm],
-        out_specs=(vm, vm),
+        out_shape=(jax.ShapeDtypeStruct((rows, d_model), bf16), jax.ShapeDtypeStruct((1, 1), jnp.int32), jax.ShapeDtypeStruct((8, rows), jnp.int32), jax.ShapeDtypeStruct((rows, 128), f32), jax.ShapeDtypeStruct((ndev // 2, 8, rows * ndev * 4 // experts), f32)),
+        in_specs=[hbm] * 5 + [vm] * 2,
+        out_specs=(vm, pl.BlockSpec(memory_space=pltpu.SMEM), vm, vm, vm),
         scratch_shapes=[
             pltpu.VMEM((ndev, rows, d_model), bf16), pltpu.VMEM((d_model, 3 * width), bf16), pltpu.VMEM((d_model, heads, head_dim), bf16), pltpu.VMEM((seq, 3 * width), bf16),
             pltpu.VMEM((heads, QB, seq), f32), pltpu.VMEM((heads, QB, head_dim), f32),
             pltpu.VMEM((seq, width), bf16), pltpu.VMEM((rows, ndev * width), bf16),
             pltpu.VMEM((ndev * width, d_model), bf16),
-            pltpu.VMEM((ndev,) + flag.shape, f32),
+            pltpu.VMEM((8, 128), f32), pltpu.VMEM((ndev, 8, 128), f32), pltpu.VMEM((128, rows), f32),
             dma((3,)), dma((18,)), dma((ndev, 4)), dma((9,)), dma((9,)), dma((16,)), dma((ndev, 2)), dma((ndev,)), dma((ndev,)),
         ],
         compiler_params=pltpu.CompilerParams(collective_id=0, has_side_effects=True, vmem_limit_bytes=63 * MIB),
         cost_estimate=pl.CostEstimate(flops=2 * seq * d_model * width * 3 + 4 * seq * seq * width, bytes_accessed=16 * MIB, transcendentals=0),
-    )(x_blk, w_q, w_k, w_v, w_o, flag)
-
-
-def moe_block(h_ref, rl_ref, rc_ref, g_ref, meta_ref, wg_hbm, wu_hbm, wd_hbm, y_ref, send, recv, zbuf, ret,
+    )(x_blk, w_q, w_k, w_v, w_o, ids, gates)
+
+
+def moe_block(h_ref, rl_ref, col_ref, meta_ref, wg_hbm, wu_hbm, wd_hbm, y_ref, send, recv, zbuf, ret,
               meta_in, sp_send, sp_recv, sp_z, sp_ret, pool_in, xs, zacc, acc, wg, wu, wd, ds, dr, rs, rr, ms, mr, sp_sem, sp_dr, pool_s, pool_r, sp_rs, sp_rr, wsem, *, main, spill):
     cp, tp = lax.axis_index('cp'), lax.axis_index('tp')
     xx, cc = tp // 2, tp % 2
@@ -400,6 +449,7 @@
     slots, _, ff_half = wg.shape
     sp_rows = sp_send.shape[1]
     sp_base = chunks * rows_all
+    c0 = 0 if spill else 2
     steps = 2 * experts
     tile = 512
     f32, bf16 = jnp.float32, jnp.bfloat16
@@ -499,7 +549,7 @@
 
     if spill:
         ids = lax.broadcasted_iota(jnp.int32, (4 * sp_rows, toks), 0) + sp_base
-        pick = ((ids == rl_ref[0:1, :]) | (ids == rl_ref[1:2, :])).astype(f32).astype(bf16)
+        pick = ((ids == rl_ref[c0:c0 + 1, :]) | (ids == rl_ref[c0 + 1:c0 + 2, :])).astype(f32).astype(bf16)
 
         def sp_cols(n, _):
             c = pl.ds(pl.multiple_of(n * tile, tile), tile)
@@ -510,7 +560,7 @@
 
     def pack(k, _):
         ids = lax.broadcasted_iota(jnp.int32, (rows_all, toks), 0) + k * rows_all
-        pick = ((ids == rl_ref[0:1, :]) | (ids == rl_ref[1:2, :])).astype(f32).astype(bf16)
+        pick = ((ids == rl_ref[c0:c0 + 1, :]) | (ids == rl_ref[c0 + 1:c0 + 2, :])).astype(f32).astype(bf16)
 
         def cols(n, _):
             c = pl.ds(pl.multiple_of(n * tile, tile), tile)
@@ -632,10 +682,12 @@
             sp_back(n).start()
         sp_home().start()
 
+    row0, row1 = (col_ref[:, c:c + 1].astype(jnp.int32) for c in (c0, c0 + 1))
+
     def chosen(ids, z):
-        z0 = jnp.dot((ids == rc_ref[:, 0:1]).astype(f32).astype(bf16), z, preferred_element_type=f32)
-        z1 = jnp.dot((ids == rc_ref[:, 1:2]).astype(f32).astype(bf16), z, preferred_element_type=f32)
-        return g_ref[:, 0:1] * z0 + g_ref[:, 1:2] * z1
+        z0 = jnp.dot((ids == row0).astype(f32).astype(bf16), z, preferred_element_type=f32)
+        z1 = jnp.dot((ids == row1).astype(f32).astype(bf16), z, preferred_element_type=f32)
+        return col_ref[:, 4:5] * z0 + col_ref[:, 5:6] * z1
 
     def combine(k, _):
         arrived(*back_way, k)
@@ -684,7 +736,7 @@
             sp_back(n).wait_send()
 
 
-def moe(hidden, rows, gates, meta, w_gate, w_up, w_down, ndev, main, spill):
+def moe(hidden, lane, col, meta, w_gate, w_up, w_down, ndev, main, spill):
     toks, d_model = hidden.shape
     experts, _, ff = w_gate.shape
     crow = 2 * main
@@ -697,12 +749,11 @@
     dma = pltpu.SemaphoreType.DMA
     buf = pltpu.VMEM((chunks, ndev, crow, d_model), bf16)
     tile_rows = 2 * ndev * main if spill else ndev * main
-    rows_lane = jnp.pad(rows.T, ((0, 6), (0, 0)), constant_values=-1)
     return pl.pallas_call(
         functools.partial(moe_block, main=main, spill=spill),
         name='moe_spill' if spill else 'moe_full',
         out_shape=jax.ShapeDtypeStruct((toks, d_model), bf16),
-        in_specs=[vm] * 5 + [hbm] * 3,
+        in_specs=[vm] * 4 + [hbm] * 3,
         out_specs=vm,
         scratch_shapes=[
             buf, buf, buf, buf, pltpu.VMEM((ndev,) + meta.shape[1:], f32),
@@ -715,7 +766,7 @@
         ],
         compiler_params=pltpu.CompilerParams(collective_id=1 if spill else 2, has_side_effects=True, vmem_limit_bytes=63 * MIB),
         cost_estimate=pl.CostEstimate(flops=6 * tile_rows * experts * d_model * ff, bytes_accessed=6 * experts * d_model * ff, transcendentals=0),
-    )(hidden, rows_lane, rows, gates, meta, w_gate, w_up, w_down)
+    )(hidden, lane, col, meta, w_gate, w_up, w_down)
 
 
 def solution(mesh):
@@ -736,36 +787,11 @@
         capacity = 4 * tok_dev // num_exp
         mean = capacity // 2
         crow = 2 * mean
-        cp_rank = lax.axis_index('cp')
-        me = cp_rank * tp_size + lax.axis_index('tp')
-
-        flat = idx_blk.reshape(-1)
-        count = flat.shape[0]
-        onehot = flat[:, None] == jnp.arange(num_exp)[None, :]
-        before = (jnp.arange(count)[:, None] > jnp.arange(count)[None, :]).astype(jnp.bfloat16)
-        ranks = jnp.dot(before, onehot.astype(jnp.bfloat16), preferred_element_type=jnp.float32)
-        pos = jnp.sum(jnp.where(onehot, ranks, 0.0), axis=1).astype(jnp.int32)
-        dest, local = flat // exp_local, flat % exp_local
-        over = pos >= mean
-        chips = num_devs // 2
-        onehot = (dest[:, None] // 2 == jnp.arange(chips)[None, :]) & over[:, None]
-        ranks = jnp.dot(before, onehot.astype(jnp.bfloat16), preferred_element_type=jnp.float32)
-        spill_pos = jnp.sum(jnp.where(onehot, ranks, 0.0), axis=1).astype(jnp.int32)
-        flag = jnp.full((8, 128), jnp.max(jnp.sum(onehot.astype(jnp.float32), axis=0)))
-        main_rows = exp_local // 2 * num_devs * crow
-        rows_spill = jnp.where(over, main_rows + dest // 2 * crow + spill_pos, ((local // 2) * num_devs + dest) * crow + (local % 2) * mean + pos)
-        rows_full = ((local // 2) * num_devs + dest) * (2 * capacity) + (local % 2) * capacity + pos
-        slot = main_rows + jnp.arange(chips * crow)
-        lane = jnp.arange(num_devs * crow)
-        code = jnp.sum(jnp.where((rows_spill[:, None] == slot[None, :]) & over[:, None], (1 + (dest % 2 * exp_local + local) * mean + pos - mean)[:, None], 0), axis=0).astype(jnp.float32)
-        meta = jnp.where(lane[None, :] // crow == me, jnp.tile(code.reshape(chips, crow), (1, num_devs)), 0.0)
-        meta = jnp.broadcast_to(meta[:, None, :], (chips, 8, num_devs * crow))
-
-        hidden, most = attention_block(x_blk, w_q, w_k, w_v, w_o.reshape(-1, d_model), flag, heads, head_dim, num_devs)
-
-        def run(rows, main, spill):
-            return lambda h: moe(h, rows.reshape(tok_dev, 2), gate_blk, meta, w_gate, w_up, w_down, num_devs, main, spill)
-
-        return lax.cond(most[0, 0] <= crow, run(rows_spill, mean, True), run(rows_full, capacity, False), hidden)
+        hidden, most, lane, col, meta = attention_block(x_blk, w_q, w_k, w_v, w_o.reshape(-1, d_model), idx_blk.T, gate_blk.T, heads, head_dim, num_devs, num_exp)
+
+        def run(main, spill):
+            return lambda h: moe(h, lane, col, meta, w_gate, w_up, w_down, num_devs, main, spill)
+
+        return lax.cond(most[0, 0] <= crow, run(mean, True), run(capacity, False), hidden)
 
     return jax.shard_map(device_fn, mesh=mesh, in_specs=(row_spec, head_spec, head_spec, head_spec, wo_spec, row_spec, row_spec, expert_spec, expert_spec, expert_spec), out_specs=row_spec, check_vma=False)

time: 266 us -> 257 us (0.966)
  local copies, waits for them, and re-layouts: 8.6 us -> 3.16 us
where the time goes in v6:
time: 257 us
  Pallas kernels  253 us (98%)
  local copies, waits for them, and re-layouts  3.16 us (1%)
    pallas_call x1, Pallas kernels, attention_block(): pl.pallas_call(functools.partial(attn_block, heads=heads, head_dim=head_d...  138 us
    pallas_call x1, Pallas kernels, moe(): pl.pallas_call(functools.partial(moe_block, main=main, spill=spill), name...  115 us

profile of v6, /device:TPU:0, one launch (start us, length us, event | category | flops | bytes accessed | tf_op | source)
XLA Modules:
  0.0 257.0 jit_solution(2763046832086653426)
XLA Ops:
  0.0 137.8 %attn_block.1 = (bf16[512,2048]{1,0:T(8,128)(2,1)}, s32[1,1]{1,0:T(1,128)}, s32[8,512]{1,0:T(8,128)S(1)}, f32[512,128]{1,0:T(8,128)S(1)}, f32[4,8,256]{2,1,0:T(8,128)S(1)}) custom-call(bf16[512,2048]{1,0:T(8,128)(2,1)} %x_hbm.1, bf16[2048,4,128]{2,1,0:T(4,128)(2,1)} %wq_hbm.1, bf16[2048,4,128]{2,1,0:T(4,128)(2,1)} %wk_hbm.1, bf16[2048,4,128]{2,1,0:T(4,128)(2,1)} %wv_hbm.1, ...), custom_call_target="tpu_custom_call" | custom-call | flops 30064771072 | bytes 16777216 | tf_op jit(solution)/shard_map/attn_block/pallas_call | solution.py:421
  138.3 115.5 %conditional.1 = (bf16[512,2048]{1,0:T(8,128)(2,1)}) conditional(s32[]{:T(128)} %bitcast.3, (bf16[512,2048]{1,0:T(8,128)(2,1)}, s32[8,512]{1,0:T(8,128)S(1)}, f32[512,128]{1,0:T(8,128)S(1)}, f32[4,8,256]{2,1,0:T(8,128)S(1)}, bf16[8,2048,1024]{2,1,0:T(8,128)(2,1)}, /*index=5*/bf16[8,2048,1024]{2,1,0:T(8,128)(2,1)}, ...), branch_computations={%region_0.0_spmd, %region_1.0_spmd} | conditional | flops 25769803776 | bytes 100663304 | solution.py:795
  138.5 115.3 %moe_spill.1 = bf16[512,2048]{1,0:T(8,128)(2,1)} custom-call(bf16[512,2048]{1,0:T(8,128)(2,1)} %get-tuple-element.43.h_ref, s32[8,512]{1,0:T(8,128)S(1)} %get-tuple-element.44.rl_ref, f32[512,128]{1,0:T(8,128)S(1)} %get-tuple-element.45.col_ref, f32[4,8,256]{2,1,0:T(8,128)S(1)} %get-tuple-element.46.meta_ref, ...), custom_call_target="tpu_custom_call" | custom-call | flops 25769803776 | bytes 100663296 | tf_op jit(solution)/shard_map/cond/branch_1_fun/moe_spill/pallas_call | solution.py:752
  253.9 3.2 %copy.16 = bf16[512,2048]{1,0:T(8,128)(2,1)} copy(bf16[512,2048]{1,0:T(8,128)(2,1)} %get-tuple-element.60) | data formatting | bytes 4194304

commit v7 on v6

--- a/solution.py
+++ b/solution.py
@@ -20,8 +20,8 @@
     return out
 
 
-def attn_block(x_hbm, wq_hbm, wk_hbm, wv_hbm, wo_hbm, ids_ref, gates_ref, h_ref, any_ref, lane_ref, col_ref, meta_ref, xbuf, wqkv_ref, w_pair, qkv, s_ref, acc_ref, o_loc, o_cat, wo_buf,
-               flag_ref, flags, tall, loc_sem, xs, xr, ws, wr, os_sem, or_sem, fs, fr, *, heads, head_dim, experts):
+def attn_block(x_hbm, wq_hbm, wk_hbm, wv_hbm, wo_hbm, ids_ref, gates_ref, h_hbm, any_ref, lane_ref, col_ref, meta_ref, xbuf, wqkv_ref, w_pair, qkv, s_ref, acc_ref, o_loc, o_cat, wo_buf,
+               flag_ref, flags, tall, h_ref, h_sem, loc_sem, xs, xr, ws, wr, os_sem, or_sem, fs, fr, *, heads, head_dim, experts):
     cp, tp = lax.axis_index('cp'), lax.axis_index('tp')
     xx, cc = tp // 2, tp % 2
     me = cp * 4 + tp
@@ -31,7 +31,8 @@
     width = heads * head_dim
     seq = ndev * rows
     wrows = wo_hbm.shape[0]
-    whalf, wquart = wrows // 2, wrows // 4
+    parts = 4
+    whalf, wpart = wrows // 2, wrows // 2 // parts
 
     def tp_of(dx, dc):
         return ((xx + dx) % 2) * 2 + (cc + dc) % 2
@@ -177,7 +178,7 @@
     for j in range(1, ndev):
         flag_copy(j).start()
 
-    w_x = [(1 + k, tp, cp * whalf + k * wquart, wquart, 1 + k, XN) for k in range(2)]
+    w_x = [(1 + k, tp, cp * whalf + k * wpart, wpart, 1 + k, XN) for k in range(parts)]
 
     def gather(p):
         base = p * half_rows
@@ -274,31 +275,46 @@
     peer_t = tp_of(1, 0)
     peer_c = tp_of(1, 1)
 
+    def w_near(k, slot, shard, target):
+        return wcopy(slot * parts + 1 + k, shard, cp * whalf + k * wpart, wpart, slot * parts + 1 + k, target)
+
+    def w_far(k, slot, shard, target):
+        return wcopy(slot * parts + 1 + k, shard, (1 - cp) * whalf + k * wpart, wpart, slot * parts + 1 + k, target)
+
     def w_pass(k):
-        wcopy(1, peer_t, cp * whalf + k * wquart, wquart, 1 + k, CN).wait_recv()
-        wcopy(3 + k, peer_t, cp * whalf + k * wquart, wquart, 3 + k, YN).start()
-        wcopy(5 + k, peer_t, cp * whalf + k * wquart, wquart, 5 + k, CN).start()
+        w_near(k, 0, peer_t, CN).wait_recv()
+        w_near(k, 1, peer_t, YN).start()
+        w_near(k, 2, peer_t, CN).start()
 
     def w_last(k):
-        wcopy(1, peer_t, (1 - cp) * whalf + k * wquart, wquart, 3 + k, CN).wait_recv()
-        wcopy(7 + k, peer_t, (1 - cp) * whalf + k * wquart, wquart, 7 + k, CN).start()
+        w_far(k, 1, peer_t, CN).wait_recv()
+        w_far(k, 3, peer_t, CN).start()
+
+    def at(i, step, *work):
+        @pl.when(i == step)
+        def _():
+            for job, k in work:
+                job(k)
 
     blocks = seq // QB
 
-    def q_step(i, _):
-        @pl.when(i == blocks // 2 - 1)
+    def block_of(step):
+        p, n = step // 4, step % 4
+        y, x = (cp + 1 - n % 2) % 2, (xx + 1 - n // 2) % 2
+        return 2 * (y + p * (3 - 2 * y)) + x
+
+    def q_step(step, _):
+        i = block_of(step)
+
+        @pl.when(step == blocks // 2 - 1)
         def _():
             late()
             for early in range(blocks // 2 - 1):
-                o_send(early)
-
-        @pl.when(i == blocks - 3)
-        def _():
-            w_pass(0)
-
-        @pl.when(i == blocks - 1)
-        def _():
-            w_pass(1)
+                o_send(block_of(early))
+
+        at(step, 5, (w_pass, 1))
+        at(step, 6, (w_pass, 3))
+        at(step, 7, (w_last, 1))
 
         q_rows = pl.ds(pl.multiple_of(i * QB, QB), QB)
 
@@ -325,6 +341,11 @@
             s_ref[h, :, pl.ds(pl.multiple_of(i * QB, QB), QB)] = s
             tops.append(jnp.max(jnp.maximum(ms[h], lane_fold(s, jnp.maximum)), axis=1, keepdims=True))
         acc_ref[...] = jnp.zeros_like(acc_ref)
+        at(step, 4, (w_pass, 0))
+        at(step, 5, (w_pass, 2))
+        at(step, 6, (w_last, 0))
+        at(step, 7, (w_last, 2))
+
 
         def pass2(j, ls):
             out = []
@@ -340,7 +361,7 @@
             total = jnp.sum(ls[h], axis=1, keepdims=True)
             o_loc[q_rows, h * head_dim:(h + 1) * head_dim] = (acc_ref[h] / total).astype(jnp.bfloat16)
 
-        @pl.when(i >= blocks // 2 - 1)
+        @pl.when(step >= blocks // 2 - 1)
         def _():
             o_send(i)
 
@@ -353,19 +374,35 @@
 
     lax.fori_loop(0, 2, phase, 0)
 
-    w_last(0)
-    w_last(1)
-    wcopy(1, tp_of(0, 1), 0, wrows, 0, CN).wait_recv()
-    for k in range(2):
-        wcopy(1, peer_c, cp * whalf + k * wquart, wquart, 5 + k, CN).wait_recv()
-        wcopy(1, peer_c, (1 - cp) * whalf + k * wquart, wquart, 7 + k, CN).wait_recv()
-    for k in range(1, ndev):
-        src = (me + k) % ndev
-        col = (4 * (src % 4) + 2 * (src // 4)) * head_dim
-        for half in range(2):
+    w_last(3)
+    wcopy(0, tp_of(0, 1), 0, wrows, 0, CN).wait_recv()
+    for k in range(parts):
+        w_near(k, 2, peer_c, CN).wait_recv()
+        w_far(k, 3, peer_c, CN).wait_recv()
+
+    def o_arrived(half):
+        for k in range(1, ndev):
+            src = (me + k) % ndev
+            col = (4 * (src % 4) + 2 * (src // 4)) * head_dim
             ref = o_cat.at[pl.ds(half * half_rows, half_rows), pl.ds(pl.multiple_of(col, width), width)]
             pltpu.make_async_remote_copy(src_ref=ref, dst_ref=ref, send_sem=os_sem.at[0], recv_sem=or_sem.at[src, half], device_id=dev(0, 0, 1), device_id_type=MESH).wait_recv()
 
+    my_seg = [cp, 3 - cp]
+    tile = 512
+    for half in range(2):
+        o_arrived(half)
+        o_local(my_seg[half] * 4 + tp).wait()
+        r = slice(half * half_rows, (half + 1) * half_rows)
+
+        def out_step(n, _):
+            c = pl.ds(pl.multiple_of(n * tile, tile), tile)
+            a = jnp.dot(o_cat[r, :], wo_buf[:, c], preferred_element_type=jnp.float32)
+            h_ref[r, c] = (xbuf[me, r, c].astype(jnp.float32) + a).astype(jnp.bfloat16)
+            return 0
+
+        lax.fori_loop(0, d_model // tile, out_step, 0)
+        pltpu.make_async_copy(h_ref.at[r], h_hbm.at[r], h_sem.at[half]).start()
+
     def drain(b, _):
         r, t, _half = o_place(b)
 
@@ -373,23 +410,9 @@
         def _():
             o_remote(b).wait_send()
 
-        @pl.when(r * 4 + t == me)
-        def _():
-            o_local(b).wait()
-
         return 0
 
     lax.fori_loop(0, seq // half_rows, drain, 0)
-
-    tile = 256
-
-    def out_step(n, _):
-        c = pl.ds(pl.multiple_of(n * tile, tile), tile)
-        a = jnp.dot(o_cat[...], wo_buf[:, c], preferred_element_type=jnp.float32)
-        h_ref[:, c] = (xbuf[me, :, c].astype(jnp.float32) + a).astype(jnp.bfloat16)
-        return 0
-
-    lax.fori_loop(0, d_model // tile, out_step, 0)
 
     most = flag_ref[...]
     for j in range(1, ndev):
@@ -404,10 +427,13 @@
     w_own.wait_send()
     for spec in w_x:
         wcopy(*spec).wait_send()
-    for k in range(2):
-        wcopy(3 + k, peer_t, cp * whalf + k * wquart, wquart, 3 + k, YN).wait_send()
-        wcopy(5 + k, peer_t, cp * whalf + k * wquart, wquart, 5 + k, CN).wait_send()
-        wcopy(7 + k, peer_t, (1 - cp) * whalf + k * wquart, wquart, 7 + k, CN).wait_send()
+    for k in range(parts):
+        w_near(k, 1, peer_t, YN).wait_send()
+        w_near(k, 2, peer_t, CN).wait_send()
+        w_far(k, 3, peer_t, CN).wait_send()
+    for half in range(2):
+        r = slice(half * half_rows, (half + 1) * half_rows)
+        pltpu.make_async_copy(h_ref.at[r], h_hbm.at[r], h_sem.at[half]).wait()
 
 
 def attention_block(x_blk, w_q, w_k, w_v, w_o, ids, gates, heads, head_dim, ndev, experts):
@@ -423,21 +449,21 @@
         name='attn_block',
         out_shape=(jax.ShapeDtypeStruct((rows, d_model), bf16), jax.ShapeDtypeStruct((1, 1), jnp.int32), jax.ShapeDtypeStruct((8, rows), jnp.int32), jax.ShapeDtypeStruct((rows, 128), f32), jax.ShapeDtypeStruct((ndev // 2, 8, rows * ndev * 4 // experts), f32)),
         in_specs=[hbm] * 5 + [vm] * 2,
-        out_specs=(vm, pl.BlockSpec(memory_space=pltpu.SMEM), vm, vm, vm),
+        out_specs=(hbm, pl.BlockSpec(memory_space=pltpu.SMEM), vm, vm, vm),
         scratch_shapes=[
             pltpu.VMEM((ndev, rows, d_model), bf16), pltpu.VMEM((d_model, 3 * width), bf16), pltpu.VMEM((d_model, heads, head_dim), bf16), pltpu.VMEM((seq, 3 * width), bf16),
             pltpu.VMEM((heads, QB, seq), f32), pltpu.VMEM((heads, QB, head_dim), f32),
             pltpu.VMEM((seq, width), bf16), pltpu.VMEM((rows, ndev * width), bf16),
             pltpu.VMEM((ndev * width, d_model), bf16),
-            pltpu.VMEM((8, 128), f32), pltpu.VMEM((ndev, 8, 128), f32), pltpu.VMEM((128, rows), f32),
-            dma((3,)), dma((18,)), dma((ndev, 4)), dma((9,)), dma((9,)), dma((16,)), dma((ndev, 2)), dma((ndev,)), dma((ndev,)),
+            pltpu.VMEM((8, 128), f32), pltpu.VMEM((ndev, 8, 128), f32), pltpu.VMEM((128, rows), f32), pltpu.VMEM((rows, d_model), bf16), dma((2,)),
+            dma((3,)), dma((18,)), dma((ndev, 4)), dma((17,)), dma((17,)), dma((16,)), dma((ndev, 2)), dma((ndev,)), dma((ndev,)),
         ],
         compiler_params=pltpu.CompilerParams(collective_id=0, has_side_effects=True, vmem_limit_bytes=63 * MIB),
         cost_estimate=pl.CostEstimate(flops=2 * seq * d_model * width * 3 + 4 * seq * seq * width, bytes_accessed=16 * MIB, transcendentals=0),
     )(x_blk, w_q, w_k, w_v, w_o, ids, gates)
 
 
-def moe_block(h_ref, rl_ref, col_ref, meta_ref, wg_hbm, wu_hbm, wd_hbm, y_ref, send, recv, zbuf, ret,
+def moe_block(h_hbm, rl_ref, col_ref, meta_ref, wg_hbm, wu_hbm, wd_hbm, y_hbm, h_ref, y_ref, io_sem, send, recv, zbuf, ret,
               meta_in, sp_send, sp_recv, sp_z, sp_ret, pool_in, xs, zacc, acc, wg, wu, wd, ds, dr, rs, rr, ms, mr, sp_sem, sp_dr, pool_s, pool_r, sp_rs, sp_rr, wsem, *, main, spill):
     cp, tp = lax.axis_index('cp'), lax.axis_index('tp')
     xx, cc = tp // 2, tp % 2
@@ -465,6 +491,8 @@
         for copy in weights(n):
             copy.start()
 
+    h_load = pltpu.make_async_copy(h_hbm, h_ref, io_sem.at[0])
+    h_load.start()
     for n in range(slots - 1):
         fetch(n)
 
@@ -547,6 +575,7 @@
     def sp_own():
         return pltpu.make_async_copy(sp_send.at[chip(0, 0)], sp_recv.at[me], sp_sem.at[7])
 
+    h_load.wait()
     if spill:
         ids = lax.broadcasted_iota(jnp.int32, (4 * sp_rows, toks), 0) + sp_base
         pick = ((ids == rl_ref[c0:c0 + 1, :]) | (ids == rl_ref[c0 + 1:c0 + 2, :])).astype(f32).astype(bf16)
@@ -557,6 +586,9 @@
             return 0
 
         lax.fori_loop(0, d_model // tile, sp_cols, 0)
+        for n in range(4):
+            sp_out(n).start()
+        sp_own().start()
 
     def pack(k, _):
         ids = lax.broadcasted_iota(jnp.int32, (rows_all, toks), 0) + k * rows_all
@@ -573,13 +605,6 @@
         @pl.when(k > 0)
         def _():
             begin(*out_way, k - 1)
-
-        if spill:
-            @pl.when(k == 0)
-            def _():
-                for n in range(4):
-                    sp_out(n).start()
-                sp_own().start()
 
         return 0
 
@@ -708,6 +733,10 @@
             ref = sp_ret.at[chip(*AWAY[n])]
             sp_copy(ref, ref, sp_rs.at[n], sp_rr.at[chip(*AWAY[n])], (0, 0, 1)).wait_recv()
 
+    def y_copy(n):
+        c = pl.ds(pl.multiple_of(n * tile, tile), tile)
+        return pltpu.make_async_copy(y_ref.at[:, c], y_hbm.at[:, c], io_sem.at[n])
+
     def finish(n, _):
         c = pl.ds(pl.multiple_of(n * tile, tile), tile)
         moe_out = acc[:, c]
@@ -715,6 +744,7 @@
             ids = lax.broadcasted_iota(jnp.int32, (toks, 4 * sp_rows), 1) + sp_base
             moe_out += chosen(ids, sp_ret[:, :, c].reshape(4 * sp_rows, tile))
         y_ref[:, c] = (h_ref[:, c].astype(f32) + moe_out).astype(bf16)
+        y_copy(n).start()
         return 0
 
     lax.fori_loop(0, d_model // tile, finish, 0)
@@ -725,6 +755,8 @@
         return 0
 
     lax.fori_loop(0, chunks, drain, 0)
+    for n in range(d_model // tile):
+        y_copy(n).wait()
     if spill:
         for j in range(1, ndev):
             meta_copy(j).wait_send()
@@ -753,9 +785,10 @@
         functools.partial(moe_block, main=main, spill=spill),
         name='moe_spill' if spill else 'moe_full',
         out_shape=jax.ShapeDtypeStruct((toks, d_model), bf16),
-        in_specs=[vm] * 4 + [hbm] * 3,
-        out_specs=vm,
+        in_specs=[hbm] + [vm] * 3 + [hbm] * 3,
+        out_specs=hbm,
         scratch_shapes=[
+            pltpu.VMEM((toks, d_model), bf16), pltpu.VMEM((toks, d_model), bf16), dma((d_model // 512,)),
             buf, buf, buf, buf, pltpu.VMEM((ndev,) + meta.shape[1:], f32),
             pltpu.VMEM((4, sp_rows, d_model), bf16), pltpu.VMEM((ndev, sp_rows, d_model), bf16), pltpu.VMEM((ndev, sp_rows, d_model), bf16),
             pltpu.VMEM((4, sp_rows, d_model), bf16), pltpu.VMEM((4, sp_rows, d_model), bf16),

time: 257 us -> 248 us (0.965)
  Pallas kernels: 253 us -> 244 us
    pallas_call x1, Pallas kernels: 138 us -> 131 us  [attention_block(): pl.pallas_call(functools.partial(attn_block, heads=heads, head_dim=head_d...]
    pallas_call x1, Pallas kernels: 115 us -> 113 us  [moe(): pl.pallas_call(functools.partial(moe_block, main=main, spill=spill), name...]
where the time goes in v7:
time: 248 us
  Pallas kernels  244 us (98%)
  local copies, waits for them, and re-layouts  3.16 us (1%)
    pallas_call x1, Pallas kernels, attention_block(): pl.pallas_call(functools.partial(attn_block, heads=heads, head_dim=head_d...  131 us
    pallas_call x1, Pallas kernels, moe(): pl.pallas_call(functools.partial(moe_block, main=main, spill=spill), name...  113 us

profile of v7, /device:TPU:0, one launch (start us, length us, event | category | flops | bytes accessed | tf_op | source)
XLA Modules:
  0.0 247.6 jit_solution(17287468529454280840)
XLA Ops:
  0.0 131.1 %attn_block.1 = (bf16[512,2048]{1,0:T(8,128)(2,1)}, s32[1,1]{1,0:T(1,128)}, s32[8,512]{1,0:T(8,128)S(1)}, f32[512,128]{1,0:T(8,128)S(1)}, f32[4,8,256]{2,1,0:T(8,128)S(1)}) custom-call(bf16[512,2048]{1,0:T(8,128)(2,1)} %x_hbm.1, bf16[2048,4,128]{2,1,0:T(4,128)(2,1)} %wq_hbm.1, bf16[2048,4,128]{2,1,0:T(4,128)(2,1)} %wk_hbm.1, bf16[2048,4,128]{2,1,0:T(4,128)(2,1)} %wv_hbm.1, ...), custom_call_target="tpu_custom_call" | custom-call | flops 30064771072 | bytes 16777216 | tf_op jit(solution)/shard_map/attn_block/pallas_call | solution.py:447
  131.7 112.8 %conditional.1 = (bf16[512,2048]{1,0:T(8,128)(2,1)}) conditional(s32[]{:T(128)} %bitcast.3, (bf16[512,2048]{1,0:T(8,128)(2,1)}, s32[8,512]{1,0:T(8,128)S(1)}, f32[512,128]{1,0:T(8,128)S(1)}, f32[4,8,256]{2,1,0:T(8,128)S(1)}, bf16[8,2048,1024]{2,1,0:T(8,128)(2,1)}, /*index=5*/bf16[8,2048,1024]{2,1,0:T(8,128)(2,1)}, ...), branch_computations={%region_0.0_spmd, %region_1.0_spmd} | conditional | flops 25769803776 | bytes 100663304 | solution.py:828
  131.9 112.6 %moe_spill.1 = bf16[512,2048]{1,0:T(8,128)(2,1)} custom-call(bf16[512,2048]{1,0:T(8,128)(2,1)} %get-tuple-element.43.h_hbm, s32[8,512]{1,0:T(8,128)S(1)} %get-tuple-element.44.rl_ref, f32[512,128]{1,0:T(8,128)S(1)} %get-tuple-element.45.col_ref, f32[4,8,256]{2,1,0:T(8,128)S(1)} %get-tuple-element.46.meta_ref, ...), custom_call_target="tpu_custom_call" | custom-call | flops 25769803776 | bytes 100663296 | tf_op jit(solution)/shard_map/cond/branch_1_fun/moe_spill/pallas_call | solution.py:784
  244.5 3.2 %copy.16 = bf16[512,2048]{1,0:T(8,128)(2,1)} copy(bf16[512,2048]{1,0:T(8,128)(2,1)} %get-tuple-element.60) | data formatting | bytes 4194304

commit v8 on v7

--- a/solution.py
+++ b/solution.py
@@ -306,14 +306,8 @@
     def q_step(step, _):
         i = block_of(step)
 
-        @pl.when(step == blocks // 2 - 1)
-        def _():
-            late()
-            for early in range(blocks // 2 - 1):
-                o_send(block_of(early))
-
-        at(step, 5, (w_pass, 1))
-        at(step, 6, (w_pass, 3))
+        at(step, 4, (w_pass, 0))
+        at(step, 5, (w_pass, 2))
         at(step, 7, (w_last, 1))
 
         q_rows = pl.ds(pl.multiple_of(i * QB, QB), QB)
@@ -341,8 +335,14 @@
             s_ref[h, :, pl.ds(pl.multiple_of(i * QB, QB), QB)] = s
             tops.append(jnp.max(jnp.maximum(ms[h], lane_fold(s, jnp.maximum)), axis=1, keepdims=True))
         acc_ref[...] = jnp.zeros_like(acc_ref)
-        at(step, 4, (w_pass, 0))
-        at(step, 5, (w_pass, 2))
+        @pl.when(step == 2)
+        def _():
+            late()
+            for early in range(2):
+                o_send(block_of(early))
+
+        at(step, 4, (w_pass, 1))
+        at(step, 5, (w_pass, 3))
         at(step, 6, (w_last, 0))
         at(step, 7, (w_last, 2))
 
@@ -361,7 +361,7 @@
             total = jnp.sum(ls[h], axis=1, keepdims=True)
             o_loc[q_rows, h * head_dim:(h + 1) * head_dim] = (acc_ref[h] / total).astype(jnp.bfloat16)
 
-        @pl.when(step >= blocks // 2 - 1)
+        @pl.when(step >= 2)
         def _():
             o_send(i)
 

time: 248 us -> 244 us (0.984)
  Pallas kernels: 244 us -> 240 us
    pallas_call x1, Pallas kernels: 131 us -> 126 us  [attention_block(): pl.pallas_call(functools.partial(attn_block, heads=heads, head_dim=head_d...]
where the time goes in v8:
time: 244 us; the launch traced here: 243 us
  Pallas kernels  240 us (98%)
  local copies, waits for them, and re-layouts  3.16 us (1%)
    pallas_call x1, Pallas kernels, attention_block(): pl.pallas_call(functools.partial(attn_block, heads=heads, head_dim=head_d...  126 us
    pallas_call x1, Pallas kernels, moe(): pl.pallas_call(functools.partial(moe_block, main=main, spill=spill), name...  114 us

profile of v8, /device:TPU:0, one launch (start us, length us, event | category | flops | bytes accessed | tf_op | source)
XLA Modules:
  0.0 243.5 jit_solution(1132860202763730220)
XLA Ops:
  0.0 126.0 %attn_block.1 = (bf16[512,2048]{1,0:T(8,128)(2,1)}, s32[1,1]{1,0:T(1,128)}, s32[8,512]{1,0:T(8,128)S(1)}, f32[512,128]{1,0:T(8,128)S(1)}, f32[4,8,256]{2,1,0:T(8,128)S(1)}) custom-call(bf16[512,2048]{1,0:T(8,128)(2,1)} %x_hbm.1, bf16[2048,4,128]{2,1,0:T(4,128)(2,1)} %wq_hbm.1, bf16[2048,4,128]{2,1,0:T(4,128)(2,1)} %wk_hbm.1, bf16[2048,4,128]{2,1,0:T(4,128)(2,1)} %wv_hbm.1, ...), custom_call_target="tpu_custom_call" | custom-call | flops 30064771072 | bytes 16777216 | tf_op jit(solution)/shard_map/attn_block/pallas_call | solution.py:447
  126.6 113.8 %conditional.1 = (bf16[512,2048]{1,0:T(8,128)(2,1)}) conditional(s32[]{:T(128)} %bitcast.3, (bf16[512,2048]{1,0:T(8,128)(2,1)}, s32[8,512]{1,0:T(8,128)S(1)}, f32[512,128]{1,0:T(8,128)S(1)}, f32[4,8,256]{2,1,0:T(8,128)S(1)}, bf16[8,2048,1024]{2,1,0:T(8,128)(2,1)}, /*index=5*/bf16[8,2048,1024]{2,1,0:T(8,128)(2,1)}, ...), branch_computations={%region_0.0_spmd, %region_1.0_spmd} | conditional | flops 25769803776 | bytes 100663304 | solution.py:828
  126.8 113.6 %moe_spill.1 = bf16[512,2048]{1,0:T(8,128)(2,1)} custom-call(bf16[512,2048]{1,0:T(8,128)(2,1)} %get-tuple-element.43.h_hbm, s32[8,512]{1,0:T(8,128)S(1)} %get-tuple-element.44.rl_ref, f32[512,128]{1,0:T(8,128)S(1)} %get-tuple-element.45.col_ref, f32[4,8,256]{2,1,0:T(8,128)S(1)} %get-tuple-element.46.meta_ref, ...), custom_call_target="tpu_custom_call" | custom-call | flops 25769803776 | bytes 100663296 | tf_op jit(solution)/shard_map/cond/branch_1_fun/moe_spill/pallas_call | solution.py:784
  240.3 3.2 %copy.16 = bf16[512,2048]{1,0:T(8,128)(2,1)} copy(bf16[512,2048]{1,0:T(8,128)(2,1)} %get-tuple-element.60) | data formatting | bytes 4194304

commit v9 on v8

--- a/solution.py
+++ b/solution.py
@@ -496,8 +496,11 @@
     for n in range(slots - 1):
         fetch(n)
 
+    order = [(0, 0, 0), (1, 0, 0), (0, 1, 0), (1, 1, 0), (1, 0, 1), (0, 1, 1), (1, 1, 1), (0, 0, 1)]
+
     def peer_of(j):
-        return (me + j) % ndev
+        dx, dy, dc = order[j]
+        return ((cp + dy) % 2) * 4 + ((xx + dx) % 2) * 2 + (cc + dc) % 2
 
     def dev(p):
         return {'cp': p // 4, 'tp': p % 4}

time: 244 us -> 244 us (level)
  no operation moved by 1% of the time
where the time goes in v9:
time: 244 us; the launch traced here: 243 us
  Pallas kernels  239 us (98%)
  local copies, waits for them, and re-layouts  3.16 us (1%)
    pallas_call x1, Pallas kernels, attention_block(): pl.pallas_call(functools.partial(attn_block, heads=heads, head_dim=head_d...  126 us
    pallas_call x1, Pallas kernels, moe(): pl.pallas_call(functools.partial(moe_block, main=main, spill=spill), name...  113 us

profile of v9, /device:TPU:0, one launch (start us, length us, event | category | flops | bytes accessed | tf_op | source)
XLA Modules:
  0.0 243.3 jit_solution(9538467556246693119)
XLA Ops:
  0.0 126.0 %attn_block.1 = (bf16[512,2048]{1,0:T(8,128)(2,1)}, s32[1,1]{1,0:T(1,128)}, s32[8,512]{1,0:T(8,128)S(1)}, f32[512,128]{1,0:T(8,128)S(1)}, f32[4,8,256]{2,1,0:T(8,128)S(1)}) custom-call(bf16[512,2048]{1,0:T(8,128)(2,1)} %x_hbm.1, bf16[2048,4,128]{2,1,0:T(4,128)(2,1)} %wq_hbm.1, bf16[2048,4,128]{2,1,0:T(4,128)(2,1)} %wk_hbm.1, bf16[2048,4,128]{2,1,0:T(4,128)(2,1)} %wv_hbm.1, ...), custom_call_target="tpu_custom_call" | custom-call | flops 30064771072 | bytes 16777216 | tf_op jit(solution)/shard_map/attn_block/pallas_call | solution.py:447
  126.6 113.6 %conditional.1 = (bf16[512,2048]{1,0:T(8,128)(2,1)}) conditional(s32[]{:T(128)} %bitcast.3, (bf16[512,2048]{1,0:T(8,128)(2,1)}, s32[8,512]{1,0:T(8,128)S(1)}, f32[512,128]{1,0:T(8,128)S(1)}, f32[4,8,256]{2,1,0:T(8,128)S(1)}, bf16[8,2048,1024]{2,1,0:T(8,128)(2,1)}, /*index=5*/bf16[8,2048,1024]{2,1,0:T(8,128)(2,1)}, ...), branch_computations={%region_0.0_spmd, %region_1.0_spmd} | conditional | flops 25769803776 | bytes 100663304 | solution.py:831
  126.8 113.4 %moe_spill.1 = bf16[512,2048]{1,0:T(8,128)(2,1)} custom-call(bf16[512,2048]{1,0:T(8,128)(2,1)} %get-tuple-element.43.h_hbm, s32[8,512]{1,0:T(8,128)S(1)} %get-tuple-element.44.rl_ref, f32[512,128]{1,0:T(8,128)S(1)} %get-tuple-element.45.col_ref, f32[4,8,256]{2,1,0:T(8,128)S(1)} %get-tuple-element.46.meta_ref, ...), custom_call_target="tpu_custom_call" | custom-call | flops 25769803776 | bytes 100663296 | tf_op jit(solution)/shard_map/cond/branch_1_fun/moe_spill/pallas_call | solution.py:787
  240.2 3.2 %copy.16 = bf16[512,2048]{1,0:T(8,128)(2,1)} copy(bf16[512,2048]{1,0:T(8,128)(2,1)} %get-tuple-element.60) | data formatting | bytes 4194304
